TPU v7x, 32 devices: a whole 2x2x4 slice. The times are simulated.
32 devices in a mesh: tm: 4 (over y, x), height: 8 (over z, core).
Axes of the slice: x: 2, y: 2, z: 4, core: 2. Of those that a mesh axis runs over, the one named last changes fastest.
Arguments:
- latent: bfloat16 [192, 2560], P(('tm', 'height')), may hold values from -9 to 9
- in_weight: bfloat16 [432, 384], replicated, may hold values from -0.3125 to 0.3125
- in_bias: float32 [384], replicated, may hold values from -3 to 3
- norm_gain: float32 [384], replicated, may hold values from 0.25 to 1.75
- norm_bias: float32 [384], replicated, may hold values from -3 to 3
- conv_weight: bfloat16 [10368, 384], replicated, may hold values from -0.0625 to 0.0625
- conv_bias: float32 [384], replicated, may hold values from -3 to 3
Outputs:
- features: bfloat16 [8, 24, 160, 384], P('tm', 'height')
All inputs are finite; a program needn't handle non-finite values.
Results may differ from a plain program's by a relative error of at most 0.0027.
Values may be sent and summed in bfloat16 or wider, within the bound.
No kernel may reach another device: no remote copies, remote signals or barrier semaphores. Data moves between devices by JAX's collectives and lax.ppermute only.
A program may use at most 128 MiB of HBM per device.

v0:
```python
import functools

import jax
import jax.numpy as jnp
from jax import lax
from jax.experimental import pallas as pl
from jax.experimental.pallas import tpu as pltpu
from jax.sharding import PartitionSpec as P

C_IN = 16
GROUPS = 32
COLS = 160
FR_DEV = 2
SEG = 16
LANES = 128
F32 = jnp.float32
BF16 = jnp.bfloat16


def band_kernel(w_ref, o_ref):
    o_ref[...] = jnp.zeros_like(o_ref)
    channels = w_ref.shape[1]
    for ab in range(9):
        for q in range(5):
            row = ab * LANES + q * C_IN
            o_ref[row : row + 3 * C_IN, q * channels : (q + 1) * channels] = w_ref[
                ab * 3 * C_IN : (ab + 1) * 3 * C_IN, :
            ]


def opened_kernel(rows, own_ref, other_ref, halo_ref, band_ref, bias_ref, o_ref, sum_ref, z_ref, zb_ref, p_ref):
    core = lax.rem(lax.axis_index("height"), 2)
    slots = 3 * rows
    per = COLS // SEG
    width = COLS * C_IN

    def spread(piece, frame, slot):
        base = pl.multiple_of((frame * slots + slot) * SEG, SEG)
        count = piece.shape[0]
        edge = jnp.zeros((count, LANES), F32)
        wide = jnp.concatenate([edge, piece.astype(F32), edge, edge], axis=1)
        for s in range(SEG):
            for half in range(2):
                start = LANES + s * per * C_IN - C_IN + half * 5 * C_IN
                lo = start // LANES * LANES
                window = wide[:, lo : lo + 2 * LANES]
                if start > lo:
                    window = pltpu.roll(window, 2 * LANES - (start - lo), 1)
                z_ref[half, pl.ds(base + s, count, stride=SEG), :] = window[:, :LANES]

    main = jnp.where(core == 0, rows, 0)
    edge_slot = jnp.where(core == 0, rows - 2, 2 * rows)
    for d in range(3):
        spread(own_ref[d], 2 * d + core, main)
        spread(other_ref[d], 2 * d + 1 - core, main)
        spread(halo_ref[0, d], 2 * d + 1 - core, edge_slot)
        spread(halo_ref[1, d], 2 * d + core, edge_slot)
    for half in range(2):
        zb_ref[half] = z_ref[half].astype(BF16)

    high = rows + 2
    block = 4 * high * SEG
    for half in range(2):
        for t in range(4):
            for a in range(3):
                for b in range(3):
                    row = ((t + a) * slots + b + rows - 2) * SEG
                    dst = half * block + t * high * SEG
                    ab = a * 3 + b
                    p_ref[dst : dst + high * SEG, ab * LANES : (ab + 1) * LANES] = zb_ref[
                        half, row : row + high * SEG, :
                    ]

    channels = bias_ref.shape[1]
    tiles = channels // LANES
    total = 5 * tiles
    sums = [jnp.zeros((8, LANES), F32) for _ in range(tiles)]
    squares = [jnp.zeros((8, LANES), F32) for _ in range(tiles)]
    for n in range(0, total, 2):
        size = min(2, total - n)
        out = jnp.dot(p_ref[...], band_ref[:, n * LANES : (n + size) * LANES], preferred_element_type=F32)
        for i in range(size):
            q, tile = (n + i) // tiles, (n + i) % tiles
            lanes = slice(tile * LANES, (tile + 1) * LANES)
            part = out[:, i * LANES : (i + 1) * LANES] + bias_ref[:, lanes]
            for half in range(2):
                rest = part[half * block : (half + 1) * block]
                o_ref[:, half * 5 + q, :, lanes] = rest.reshape(4 * high, SEG, LANES)
                for t in range(2, 4):
                    begin = (t * high + 1) * SEG
                    mine = rest[begin : begin + rows * SEG].reshape(-1, 8, LANES)
                    sums[tile] = sums[tile] + jnp.sum(mine, axis=0)
                    squares[tile] = squares[tile] + jnp.sum(mine * mine, axis=0)
    for tile in range(tiles):
        lanes = slice(tile * LANES, (tile + 1) * LANES)
        sum_ref[0:1, lanes] = jnp.sum(sums[tile], axis=0, keepdims=True)
        sum_ref[1:2, lanes] = jnp.sum(squares[tile], axis=0, keepdims=True)


def second_kernel(rows, entries, sum_ref, o_ref, w_ref, gain_ref, shift_ref, bias_ref, out_ref, a_ref, f_ref):
    channels = gain_ref.shape[1]
    per = COLS // SEG
    high = rows + 2
    height = lax.axis_index("height")
    frame = lax.axis_index("tm")
    group = channels // GROUPS
    left = jnp.floor((lax.broadcasted_iota(jnp.int32, (channels, channels), 0).astype(F32) + 0.5) / group)
    right = jnp.floor((lax.broadcasted_iota(jnp.int32, (channels, channels), 1).astype(F32) + 0.5) / group)
    same = jnp.where(left == right, 1.0, 0.0).astype(F32)
    totals = jnp.dot(
        jnp.concatenate([sum_ref[...], jnp.zeros((6, channels), F32)], axis=0),
        same,
        precision=lax.Precision.HIGHEST,
        preferred_element_type=F32,
    )
    mean = totals[0:1] / entries
    var = totals[1:2] / entries - mean * mean
    scale = lax.rsqrt(var + 1e-06) * gain_ref[...]
    half_scale = 0.5 * scale
    half_shift = 0.5 * (shift_ref[...] - mean * scale)

    def act(index, carry):
        t = index // high
        h = index - t * high
        row = height * rows - 1 + h
        inside = (frame * FR_DEV - 2 + t >= 0) & (row >= 0) & (row < rows * lax.axis_size("height"))
        u = o_ref[index].reshape(per * SEG, channels) * half_scale + half_shift
        y = u + u * jnp.tanh(u)
        y = jnp.where(inside, y, 0.0)
        a_ref[index, 1 : per + 1] = y.astype(BF16).reshape(per, SEG, channels)
        lane_row = lax.broadcasted_iota(jnp.int32, (SEG, channels), 0)
        before = jnp.where(lane_row == 0, 0.0, pltpu.roll(y[(per - 1) * SEG :], 1, 0))
        after = jnp.where(lane_row == SEG - 1, 0.0, pltpu.roll(y[:SEG], SEG - 1, 0))
        a_ref[index, 0] = before.astype(BF16)
        a_ref[index, per + 1] = after.astype(BF16)
        return carry

    lax.fori_loop(0, 4 * high, act, 0)

    for t in range(2):

        def patch(tap):
            a, b, c = tap // 9, tap // 3 % 3, tap % 3
            start = (t + a) * high + b
            return a_ref[start : start + rows, c : c + per].reshape(rows * per * SEG, channels)

        acc = jnp.zeros((rows * per * SEG, channels), F32)
        for tap in range(0, 27, 2):
            taps = range(tap, min(tap + 2, 27))
            lhs = jnp.concatenate([patch(x) for x in taps], axis=1) if len(taps) > 1 else patch(tap)
            rhs = w_ref[tap * channels : (taps[-1] + 1) * channels, :]
            acc = acc + jnp.dot(lhs, rhs, preferred_element_type=F32)
        acc = acc + bias_ref[...]
        for h in range(rows):
            index = (t + 2) * high + h + 1
            whole = acc[h * per * SEG : (h + 1) * per * SEG] + o_ref[index].reshape(per * SEG, channels)
            for k in range(per):
                for tile in range(channels // LANES):
                    lanes = slice(tile * LANES, (tile + 1) * LANES)
                    f_ref[tile, pl.ds(k, SEG, stride=per), :] = whole[k * SEG : (k + 1) * SEG, lanes]
            for tile in range(channels // LANES):
                out_ref[t, h, :, tile * LANES : (tile + 1) * LANES] = f_ref[tile].astype(BF16)


def pairwise_sum(x, axis):
    size = lax.axis_size(axis)
    if size & (size - 1):
        return lax.psum(x, axis)
    step = 1
    while step < size:
        x = x + lax.ppermute(x, axis, [(i, i ^ step) for i in range(size)])
        step *= 2
    return x


def shards(latent, in_weight, in_bias, norm_gain, norm_bias, conv_weight, conv_bias):
    frames = FR_DEV
    rows = latent.shape[0] // frames
    channels = conv_weight.shape[1]
    tm, height = lax.axis_size("tm"), lax.axis_size("height")
    half = height // 2
    core = lax.axis_index("height") % 2
    band = pl.pallas_call(
        band_kernel, out_shape=jax.ShapeDtypeStruct((9 * LANES, 5 * channels), BF16), name="band"
    )(in_weight)

    received = []
    for d in (2, 1, 0):
        route = [
            (i * height + p * half + m, (i + d) * height + 2 * m + p)
            for i in range(tm - d)
            for p in range(2)
            for m in range(half)
        ]
        received.append(lax.ppermute(latent, ("tm", "height"), route))
    own = jnp.stack(received)
    other = lax.ppermute(own, "height", [(i, i ^ 1) for i in range(height)])
    edge = lax.dynamic_slice_in_dim(jnp.stack([own, other]), core * (2 * rows - 2), 2, axis=2)
    swap = [(2 * m - 1, 2 * m) for m in range(1, half)] + [(2 * m, 2 * m - 1) for m in range(1, half)]
    halo = lax.ppermute(edge, "height", swap)

    per = COLS // SEG
    high = rows + 2
    slots = 3 * rows
    opened, sums = pl.pallas_call(
        functools.partial(opened_kernel, rows),
        out_shape=(
            jax.ShapeDtypeStruct((4 * high, per, SEG, channels), F32),
            jax.ShapeDtypeStruct((2, channels), F32),
        ),
        scratch_shapes=[
            pltpu.VMEM((2, 6 * slots * SEG, LANES), F32),
            pltpu.VMEM((2, 6 * slots * SEG, LANES), BF16),
            pltpu.VMEM((8 * high * SEG, 9 * LANES), BF16),
        ],
        compiler_params=pltpu.CompilerParams(vmem_limit_bytes=24 << 20),
        name="opened",
    )(own, other, halo, band, in_bias[None])
    for axis in ("height", "tm"):
        sums = pairwise_sum(sums, axis)
    entries = frames * tm * rows * height * COLS * (channels // GROUPS)
    return pl.pallas_call(
        functools.partial(second_kernel, rows, entries),
        out_shape=jax.ShapeDtypeStruct((frames, rows, COLS, channels), BF16),
        scratch_shapes=[
            pltpu.VMEM((4 * high, per + 2, SEG, channels), BF16),
            pltpu.VMEM((channels // LANES, COLS, LANES), F32),
        ],
        compiler_params=pltpu.CompilerParams(vmem_limit_bytes=32 << 20),
        name="second",
    )(sums, opened, conv_weight, norm_gain[None], norm_bias[None], conv_bias[None])


def solution(mesh):
    return jax.shard_map(
        shards,
        mesh=mesh,
        in_specs=(P(("tm", "height"), None), P(), P(), P(), P(), P(), P()),
        out_specs=P("tm", "height", None, None),
        check_vma=False,
    )
```

profile of v0, /device:TPU:0, one launch (start us, length us, event | category | flops | bytes accessed | tf_op | source)
XLA Modules:
  0.0 63.6 jit_solution(14526816641574583841)
XLA Ops:
  0.0 0.0 copy-start.2
  0.0 5.0 %collective-permute-start = (bf16[6,2560]{1,0:T(8,128)(2,1)}, bf16[6,2560]{1,0:T(8,128)(2,1)S(1)}, u32[]{:S(2)}, u32[]{:S(2)}) collective-permute-start(bf16[6,2560]{1,0:T(8,128)(2,1)} %param.7), channel_id=1, source_target_pairs={{0,16},{1,18},{2,20},{3,22},{4,17},{5,19},{6,21},{7,23},{8,24},{9,... | collective-permute-start | bytes 92168 | tf_op jit(solution)/shard_map/ppermute | solution.py:195
  5.0 3.4 %collective-permute-start.1 = (bf16[6,2560]{1,0:T(8,128)(2,1)}, bf16[6,2560]{1,0:T(8,128)(2,1)S(1)}, u32[]{:S(2)}, u32[]{:S(2)}) collective-permute-start(bf16[6,2560]{1,0:T(8,128)(2,1)} %param.7), channel_id=1, source_target_pairs={{0,8},{1,10},{2,12},{3,14},{4,9},{5,11},{6,13},{7,15},{8,16},{9,18... | collective-permute-start | bytes 92168 | tf_op jit(solution)/shard_map/ppermute | solution.py:195
  8.4 1.4 %collective-permute-start.2 = (bf16[6,2560]{1,0:T(8,128)(2,1)}, bf16[6,2560]{1,0:T(8,128)(2,1)S(1)}, u32[]{:S(2)}, u32[]{:S(2)}) collective-permute-start(bf16[6,2560]{1,0:T(8,128)(2,1)} %param.7), channel_id=1, source_target_pairs={{0,0},{1,2},{2,4},{3,6},{4,1},{5,3},{6,5},{7,7},{8,8},{9,10},{10,1... | collective-permute-start | bytes 92168 | tf_op jit(solution)/shard_map/ppermute | solution.py:195
  9.9 0.0 collective-permute-done
  9.9 0.5 collective-permute-done.1
  10.4 0.0 collective-permute-done.2
  10.4 6.7 %collective-permute-start.3 = (bf16[3,6,2560]{2,1,0:T(8,128)(2,1)S(1)}, bf16[3,6,2560]{2,1,0:T(8,128)(2,1)S(1)}, u32[]{:S(2)}, u32[]{:S(2)}) collective-permute-start(bf16[3,6,2560]{2,1,0:T(8,128)(2,1)S(1)} %get-tuple-element.10.own_ref), channel_id=1, source_target_pairs={{0,1},{1,0},{2,3},{3,2},{4,5},{5,4},{6,7},{7,6},{8,9},{9,8},{10,11... | collective-permute-start | bytes 276488 | tf_op jit(solution)/shard_map/ppermute | solution.py:197
  17.1 1.0 %collective-permute-done.3.other_ref = bf16[3,6,2560]{2,1,0:T(8,128)(2,1)S(1)} collective-permute-done((bf16[3,6,2560]{2,1,0:T(8,128)(2,1)S(1)}, bf16[3,6,2560]{2,1,0:T(8,128)(2,1)S(1)}, u32[]{:S(2)}, u32[]{:S(2)}) %collective-permute-start.3) | collective-permute-done | bytes 92192 | tf_op jit(solution)/shard_map/ppermute | solution.py:197
  18.1 0.1 fusion
  18.2 0.7 %collective-permute-start.4 = (bf16[2,3,2,2560]{3,2,1,0:T(2,128)(2,1)S(1)}, bf16[2,3,2,2560]{3,2,1,0:T(2,128)(2,1)S(1)}, u32[]{:S(2)}, u32[]{:S(2)}) collective-permute-start(bf16[2,3,2,2560]{3,2,1,0:T(2,128)(2,1)S(1)} %fusion), channel_id=1, source_target_pairs={{1,2},{3,4},{5,6},{2,1},{4,3},{6,5},{9,10},{11,12},{13,14},{10,9},... | collective-permute-start | bytes 184328 | tf_op jit(solution)/shard_map/ppermute | solution.py:200
  18.9 3.4 %band.1.band_ref = bf16[1152,1920]{1,0:T(8,128)(2,1)} custom-call(bf16[432,384]{1,0:T(8,128)(2,1)} %w_ref.2), custom_call_target="tpu_custom_call" | custom-call | tf_op jit(solution)/shard_map/band/pallas_call | solution.py:183
  22.3 0.0 copy-done.2
  22.3 0.0 collective-permute-done.4.halo_ref
  22.3 0.0 copy-start
  22.3 2.2 %copy-done = bf16[1152,1920]{1,0:T(8,128)(2,1)S(1)} copy-done((bf16[1152,1920]{1,0:T(8,128)(2,1)S(1)}, bf16[1152,1920]{1,0:T(8,128)(2,1)}, u32[]{:S(2)}) %copy-start) | copy-done | bytes 4423704
  24.5 4.2 %opened.1 = (f32[20,10,16,384]{3,2,1,0:T(8,128)S(1)}, f32[2,384]{1,0:T(2,128)S(1)}) custom-call(bf16[3,6,2560]{2,1,0:T(8,128)(2,1)S(1)} %get-tuple-element.10.own_ref, bf16[3,6,2560]{2,1,0:T(8,128)(2,1)S(1)} %collective-permute-done.3.other_ref, bf16[2,3,2,2560]{3,2,1,0:T(2,128)(2,1)S(1)} %collective-permute-done.4.halo_ref, bf16[1152,1920]{1,0:T(8,128)(2,1)S(1)} %copy-done, ...), custom_call_target="tpu_custom_call" | custom-call | tf_op jit(solution)/shard_map/opened/pallas_call | solution.py:205
  28.7 1.9 %collective-permute-start.5 = (f32[2,384]{1,0:T(2,128)S(1)}, f32[2,384]{1,0:T(2,128)S(1)}, u32[]{:S(2)}, u32[]{:S(2)}) collective-permute-start(f32[2,384]{1,0:T(2,128)S(1)} %get-tuple-element.7), channel_id=1, source_target_pairs={{0,1},{1,0},{2,3},{3,2},{4,5},{5,4},{6,7},{7,6},{8,9},{9,8},{10,11... | collective-permute-start | bytes 9224 | tf_op jit(solution)/shard_map/ppermute | solution.py:171
  30.6 0.8 %collective-permute-done.5 = f32[2,384]{1,0:T(2,128)S(1)} collective-permute-done((f32[2,384]{1,0:T(2,128)S(1)}, f32[2,384]{1,0:T(2,128)S(1)}, u32[]{:S(2)}, u32[]{:S(2)}) %collective-permute-start.5) | collective-permute-done | bytes 3104 | tf_op jit(solution)/shard_map/ppermute | solution.py:171
  31.4 1.8 %collective-permute-start.6 = (f32[2,384]{1,0:T(2,128)S(1)}, f32[2,384]{1,0:T(2,128)S(1)}, u32[]{:S(2)}, u32[]{:S(2)}) collective-permute-start(f32[2,384]{1,0:T(2,128)S(1)} %add.24), channel_id=1, source_target_pairs={{0,2},{1,3},{2,0},{3,1},{4,6},{5,7},{6,4},{7,5},{8,10},{9,11},{10,... | collective-permute-start | bytes 9224 | tf_op jit(solution)/shard_map/ppermute | solution.py:171
  33.2 1.8 %collective-permute-done.6 = f32[2,384]{1,0:T(2,128)S(1)} collective-permute-done((f32[2,384]{1,0:T(2,128)S(1)}, f32[2,384]{1,0:T(2,128)S(1)}, u32[]{:S(2)}, u32[]{:S(2)}) %collective-permute-start.6) | collective-permute-done | bytes 3104 | tf_op jit(solution)/shard_map/ppermute | solution.py:171
  35.0 1.3 %collective-permute-start.7 = (f32[2,384]{1,0:T(2,128)S(1)}, f32[2,384]{1,0:T(2,128)S(1)}, u32[]{:S(2)}, u32[]{:S(2)}) collective-permute-start(f32[2,384]{1,0:T(2,128)S(1)} %add.25), channel_id=1, source_target_pairs={{0,4},{1,5},{2,6},{3,7},{4,0},{5,1},{6,2},{7,3},{8,12},{9,13},{10,... | collective-permute-start | bytes 9224 | tf_op jit(solution)/shard_map/ppermute | solution.py:171
  36.3 3.2 %collective-permute-done.7 = f32[2,384]{1,0:T(2,128)S(1)} collective-permute-done((f32[2,384]{1,0:T(2,128)S(1)}, f32[2,384]{1,0:T(2,128)S(1)}, u32[]{:S(2)}, u32[]{:S(2)}) %collective-permute-start.7) | collective-permute-done | bytes 3104 | tf_op jit(solution)/shard_map/ppermute | solution.py:171
  39.5 0.0 collective-permute-start.8
  39.5 3.6 %collective-permute-done.8 = f32[2,384]{1,0:T(2,128)S(1)} collective-permute-done((f32[2,384]{1,0:T(2,128)S(1)}, f32[2,384]{1,0:T(2,128)S(1)}, u32[]{:S(2)}, u32[]{:S(2)}) %collective-permute-start.8) | collective-permute-done | bytes 3104 | tf_op jit(solution)/shard_map/ppermute | solution.py:171
  43.1 0.0 collective-permute-start.9
  43.1 0.0 copy-done.3
  43.1 0.0 copy-done.4
  43.2 0.0 copy-done.5
  43.2 3.5 %collective-permute-done.9 = f32[2,384]{1,0:T(2,128)S(1)} collective-permute-done((f32[2,384]{1,0:T(2,128)S(1)}, f32[2,384]{1,0:T(2,128)S(1)}, u32[]{:S(2)}, u32[]{:S(2)}) %collective-permute-start.9) | collective-permute-done | bytes 3104 | tf_op jit(solution)/shard_map/ppermute | solution.py:171
  46.7 3.3 %copy-done.1 = bf16[10368,384]{1,0:T(8,128)(2,1)S(1)} copy-done((bf16[10368,384]{1,0:T(8,128)(2,1)S(1)}, bf16[10368,384]{1,0:T(8,128)(2,1)}, u32[]{:S(2)}) %copy-start.1) | copy-done | bytes 7962648
  50.0 13.7 %second.1 = bf16[2,3,160,384]{3,2,1,0:T(8,128)(2,1)} custom-call(f32[2,384]{1,0:T(2,128)S(1)} %add.28.sum_ref, f32[20,10,16,384]{3,2,1,0:T(8,128)S(1)} %get-tuple-element.8.o_ref, bf16[10368,384]{1,0:T(8,128)(2,1)S(1)} %copy-done.1, f32[1,384]{1,0:T(1,128)S(1)} %broadcast_in_dim.13.gain_ref, f32[1,384]{1,0:T(1,128)S(1)} %broadcast_in_dim.14.shift_ref, ...), custom_call_target="tpu_custom_call" | custom-call | tf_op jit(solution)/shard_map/second/pallas_call | solution.py:222
  (14 shorter events, 0.1 us)
Async XLA Ops:
  0.0 22.3 %copy-start.2 = (f32[384]{0:T(512)S(1)}, f32[384]{0:T(512)}, u32[]{:S(2)}) copy-start(f32[384]{0:T(512)} %param.9) | copy-start | bytes 4612
  0.0 9.9 %collective-permute-start = (bf16[6,2560]{1,0:T(8,128)(2,1)}, bf16[6,2560]{1,0:T(8,128)(2,1)S(1)}, u32[]{:S(2)}, u32[]{:S(2)}) collective-permute-start(bf16[6,2560]{1,0:T(8,128)(2,1)} %param.7), channel_id=1, source_target_pairs={{0,16},{1,18},{2,20},{3,22},{4,17},{5,19},{6,21},{7,23},{8,24},{9,... | collective-permute-start | bytes 92168 | tf_op jit(solution)/shard_map/ppermute | solution.py:195
  5.0 5.4 %collective-permute-start.1 = (bf16[6,2560]{1,0:T(8,128)(2,1)}, bf16[6,2560]{1,0:T(8,128)(2,1)S(1)}, u32[]{:S(2)}, u32[]{:S(2)}) collective-permute-start(bf16[6,2560]{1,0:T(8,128)(2,1)} %param.7), channel_id=1, source_target_pairs={{0,8},{1,10},{2,12},{3,14},{4,9},{5,11},{6,13},{7,15},{8,16},{9,18... | collective-permute-start | bytes 92168 | tf_op jit(solution)/shard_map/ppermute | solution.py:195
  8.4 2.0 %collective-permute-start.2 = (bf16[6,2560]{1,0:T(8,128)(2,1)}, bf16[6,2560]{1,0:T(8,128)(2,1)S(1)}, u32[]{:S(2)}, u32[]{:S(2)}) collective-permute-start(bf16[6,2560]{1,0:T(8,128)(2,1)} %param.7), channel_id=1, source_target_pairs={{0,0},{1,2},{2,4},{3,6},{4,1},{5,3},{6,5},{7,7},{8,8},{9,10},{10,1... | collective-permute-start | bytes 92168 | tf_op jit(solution)/shard_map/ppermute | solution.py:195
  10.4 7.6 %collective-permute-start.3 = (bf16[3,6,2560]{2,1,0:T(8,128)(2,1)S(1)}, bf16[3,6,2560]{2,1,0:T(8,128)(2,1)S(1)}, u32[]{:S(2)}, u32[]{:S(2)}) collective-permute-start(bf16[3,6,2560]{2,1,0:T(8,128)(2,1)S(1)} %get-tuple-element.10.own_ref), channel_id=1, source_target_pairs={{0,1},{1,0},{2,3},{3,2},{4,5},{5,4},{6,7},{7,6},{8,9},{9,8},{10,11... | collective-permute-start | bytes 276488 | tf_op jit(solution)/shard_map/ppermute | solution.py:197
  18.1 25.0 %copy-start.3 = (f32[384]{0:T(512)S(1)}, f32[384]{0:T(512)}, u32[]{:S(2)}) copy-start(f32[384]{0:T(512)} %param.10) | copy-start | bytes 4612
  18.1 25.1 %copy-start.4 = (f32[384]{0:T(512)S(1)}, f32[384]{0:T(512)}, u32[]{:S(2)}) copy-start(f32[384]{0:T(512)} %param.11) | copy-start | bytes 4612
  18.1 25.1 %copy-start.5 = (f32[384]{0:T(512)S(1)}, f32[384]{0:T(512)}, u32[]{:S(2)}) copy-start(f32[384]{0:T(512)} %param.13) | copy-start | bytes 4612
  18.2 4.1 %collective-permute-start.4 = (bf16[2,3,2,2560]{3,2,1,0:T(2,128)(2,1)S(1)}, bf16[2,3,2,2560]{3,2,1,0:T(2,128)(2,1)S(1)}, u32[]{:S(2)}, u32[]{:S(2)}) collective-permute-start(bf16[2,3,2,2560]{3,2,1,0:T(2,128)(2,1)S(1)} %fusion), channel_id=1, source_target_pairs={{1,2},{3,4},{5,6},{2,1},{4,3},{6,5},{9,10},{11,12},{13,14},{10,9},... | collective-permute-start | bytes 184328 | tf_op jit(solution)/shard_map/ppermute | solution.py:200
  22.3 2.3 %copy-start = (bf16[1152,1920]{1,0:T(8,128)(2,1)S(1)}, bf16[1152,1920]{1,0:T(8,128)(2,1)}, u32[]{:S(2)}) copy-start(bf16[1152,1920]{1,0:T(8,128)(2,1)} %band.1.band_ref) | copy-start | bytes 13271044
  28.7 2.7 %collective-permute-start.5 = (f32[2,384]{1,0:T(2,128)S(1)}, f32[2,384]{1,0:T(2,128)S(1)}, u32[]{:S(2)}, u32[]{:S(2)}) collective-permute-start(f32[2,384]{1,0:T(2,128)S(1)} %get-tuple-element.7), channel_id=1, source_target_pairs={{0,1},{1,0},{2,3},{3,2},{4,5},{5,4},{6,7},{7,6},{8,9},{9,8},{10,11... | collective-permute-start | bytes 9224 | tf_op jit(solution)/shard_map/ppermute | solution.py:171
  31.4 3.6 %collective-permute-start.6 = (f32[2,384]{1,0:T(2,128)S(1)}, f32[2,384]{1,0:T(2,128)S(1)}, u32[]{:S(2)}, u32[]{:S(2)}) collective-permute-start(f32[2,384]{1,0:T(2,128)S(1)} %add.24), channel_id=1, source_target_pairs={{0,2},{1,3},{2,0},{3,1},{4,6},{5,7},{6,4},{7,5},{8,10},{9,11},{10,... | collective-permute-start | bytes 9224 | tf_op jit(solution)/shard_map/ppermute | solution.py:171
  35.0 4.5 %collective-permute-start.7 = (f32[2,384]{1,0:T(2,128)S(1)}, f32[2,384]{1,0:T(2,128)S(1)}, u32[]{:S(2)}, u32[]{:S(2)}) collective-permute-start(f32[2,384]{1,0:T(2,128)S(1)} %add.25), channel_id=1, source_target_pairs={{0,4},{1,5},{2,6},{3,7},{4,0},{5,1},{6,2},{7,3},{8,12},{9,13},{10,... | collective-permute-start | bytes 9224 | tf_op jit(solution)/shard_map/ppermute | solution.py:171
  39.5 3.6 %collective-permute-start.8 = (f32[2,384]{1,0:T(2,128)S(1)}, f32[2,384]{1,0:T(2,128)S(1)}, u32[]{:S(2)}, u32[]{:S(2)}) collective-permute-start(f32[2,384]{1,0:T(2,128)S(1)} %add.26), channel_id=1, source_target_pairs={{0,8},{8,0},{16,24},{24,16},{1,9},{9,1},{17,25},{25,17},{2,10},{10... | collective-permute-start | bytes 9224 | tf_op jit(solution)/shard_map/ppermute | solution.py:171
  43.1 3.6 %collective-permute-start.9 = (f32[2,384]{1,0:T(2,128)S(1)}, f32[2,384]{1,0:T(2,128)S(1)}, u32[]{:S(2)}, u32[]{:S(2)}) collective-permute-start(f32[2,384]{1,0:T(2,128)S(1)} %add.27), channel_id=1, source_target_pairs={{0,16},{8,24},{16,0},{24,8},{1,17},{9,25},{17,1},{25,9},{2,18},{10... | collective-permute-start | bytes 9224 | tf_op jit(solution)/shard_map/ppermute | solution.py:171
  46.7 3.3 %copy-start.1 = (bf16[10368,384]{1,0:T(8,128)(2,1)S(1)}, bf16[10368,384]{1,0:T(8,128)(2,1)}, u32[]{:S(2)}) copy-start(bf16[10368,384]{1,0:T(8,128)(2,1)} %w_ref.3) | copy-start | bytes 23887876
where the time goes:
time: 64 us; the launch traced here: 63.6 us
  starting transfers between devices  22.1 us (35%)
  Pallas kernels  21.3 us (33%)
  waiting for transfers between devices  14.5 us (23%)
  local copies, waits for them, and re-layouts  5.53 us (9%)
    pallas_call x1, Pallas kernels, shards(): pl.pallas_call(functools.partial(second_kernel, rows, entries), out_shape...  13.7 us
    ppermute x5, waiting for transfers between devices, pairwise_sum(): x = x + lax.ppermute(x, axis, [(i, i ^ step) for i in range(size)])  13 us
    ppermute x3, starting transfers between devices, shards(): received.append(lax.ppermute(latent, ('tm', 'height'), route))  9.85 us
    ppermute x1, starting transfers between devices, shards(): other = lax.ppermute(own, 'height', [(i, i ^ 1) for i in range(height)])  6.66 us
    unnamed x12, local copies, waits for them, and re-layouts  5.52 us
    ppermute x5, starting transfers between devices, pairwise_sum(): x = x + lax.ppermute(x, axis, [(i, i ^ step) for i in range(size)])  4.94 us
    pallas_call x1, Pallas kernels, shards(): pl.pallas_call(functools.partial(opened_kernel, rows), out_shape=(jax.Sha...  4.17 us
    pallas_call x1, Pallas kernels, shards(): pl.pallas_call(band_kernel, out_shape=jax.ShapeDtypeStruct((9 * LANES, 5...  3.42 us
  transfers between devices with their start and end apart: 10, of which 7 were waited for; matrix products, arithmetic and copies ran while one was open for 0% of the time, Pallas kernels for 5%

commit v1 on v0

v1 whole, which is shorter than its diff:
```python
import functools

import jax
import jax.numpy as jnp
from jax import lax
from jax.experimental import pallas as pl
from jax.experimental.pallas import tpu as pltpu
from jax.sharding import PartitionSpec as P

C_IN = 16
GROUPS = 32
COLS = 160
FR_DEV = 2
SEG = 16
LANES = 128
F32 = jnp.float32
BF16 = jnp.bfloat16


def band_kernel(w_ref, *refs):
    *vectors, o_ref, v_ref = refs
    for i, vector in enumerate(vectors):
        v_ref[i : i + 1, :] = vector[...].reshape(1, -1)
    o_ref[...] = jnp.zeros_like(o_ref)
    channels = w_ref.shape[1]
    depth = 3 * C_IN
    places = [(a, b, a, b) for a in range(3) for b in range(2)] + [(0, 2, 3, 0), (1, 2, 3, 1), (2, 2, 4, 0)]
    for a, b, group, side in places:
        for e in range(2):
            row = group * LANES + side * (LANES // 2) + e * C_IN
            tap = (a * 3 + b) * depth
            o_ref[row : row + depth, e * channels : (e + 1) * channels] = w_ref[tap : tap + depth, :]


def windows(e_ref, f_ref, pair, frames, high):
    (t0, t1), (h0, h1) = frames, high
    rows = slice(h0 * SEG, h1 * SEG)
    parts = [e_ref[pair, t0 + a : t1 + a, rows] for a in range(3)]
    parts.append(f_ref[pair, t0:t1, rows])
    parts.append(e_ref[pair, t0 + 2 : t1 + 2, (h0 + 2) * SEG : (h1 + 2) * SEG])
    size = (t1 - t0) * (h1 - h0) * SEG
    return jnp.concatenate([part.reshape(size, LANES) for part in parts], axis=1)


def fetch(sem, *pairs):
    copies = [pltpu.make_async_copy(source, target, sem.at[i]) for i, (source, target) in enumerate(pairs)]
    for copy in copies:
        copy.start()
    return copies


def stats_kernel(
    rows, own_ref, other_ref, halo_ref, band_hbm, v_hbm, e_hbm, f_hbm, sum_ref, z_ref, band_ref, v_ref, e_ref, f_ref, sem
):
    loads = fetch(sem.at[0], (band_hbm, band_ref), (v_hbm, v_ref))
    core = lax.rem(lax.axis_index("height"), 2)
    slots = 3 * rows
    per = COLS // SEG
    high = rows + 2

    for frame in range(6):
        for slot in (0, slots - 1):
            row = (frame * slots + slot) * SEG
            for half in range(2):
                z_ref[half, row : row + SEG, :] = jnp.zeros((SEG, LANES), F32)

    def spread(piece, frame, slot):
        base = pl.multiple_of((frame * slots + slot) * SEG, SEG)
        count = piece.shape[0]
        edge = jnp.zeros((count, LANES), F32)
        wide = jnp.concatenate([edge, piece.astype(F32), edge, edge], axis=1)
        for s in range(SEG):
            for half in range(2):
                start = LANES + s * per * C_IN - C_IN + half * 6 * C_IN
                lo = start // LANES * LANES
                window = wide[:, lo : lo + 2 * LANES]
                if start > lo:
                    window = pltpu.roll(window, 2 * LANES - (start - lo), 1)
                z_ref[half, pl.ds(base + s, count, stride=SEG), :] = window[:, :LANES]

    main = jnp.where(core == 0, rows, 0)
    edge_slot = jnp.where(core == 0, rows - 2, 2 * rows)
    for d in range(3):
        spread(own_ref[d], 2 * d + core, main)
        spread(other_ref[d], 2 * d + 1 - core, main)
        spread(halo_ref[0, d], 2 * d + 1 - core, edge_slot)
        spread(halo_ref[1, d], 2 * d + core, edge_slot)

    first = rows - 2
    span = rows + 4
    low_side = lax.broadcasted_iota(jnp.int32, (span * SEG, LANES), 1) < LANES // 2
    where = [(0, 0), (0, 2 * C_IN), (0, 4 * C_IN), (1, 0), (1, 2 * C_IN)]

    def turned(x, shift):
        return x if shift % LANES == 0 else pltpu.roll(x, shift % LANES, 1)

    for pair, (half, offset) in enumerate(where):
        upper = []
        for frame in range(6):
            x = z_ref[half, pl.ds((frame * slots + first) * SEG, (span + 1) * SEG), :]
            low, up = turned(x, -offset), turned(x, LANES // 2 - offset)
            e_ref[pair, frame] = jnp.where(low_side, low[: span * SEG], up[SEG:]).astype(BF16)
            if 0 < frame < 5:
                f_ref[pair, frame - 1] = jnp.where(
                    low_side[: high * SEG], upper, up[2 * SEG : span * SEG]
                ).astype(BF16)
            upper = low[2 * SEG : span * SEG]

    channels = v_ref.shape[1]
    sums = jnp.zeros((8, 2 * channels), F32)
    squares = jnp.zeros((8, 2 * channels), F32)
    stores = fetch(sem.at[1], (e_ref, e_hbm), (f_ref, f_hbm))
    for load in loads:
        load.wait()
    bias = jnp.concatenate([v_ref[0:1, :], v_ref[0:1, :]], axis=1)
    for pair in range(per // 2):
        out = jnp.dot(
            windows(e_ref, f_ref, pair, (2, 4), (1, 1 + rows)), band_ref[...], preferred_element_type=F32
        )
        out = (out + bias).reshape(-1, 8, 2 * channels)
        sums = sums + jnp.sum(out, axis=0)
        squares = squares + jnp.sum(out * out, axis=0)
    for i, part in enumerate((sums, squares)):
        whole = jnp.sum(part, axis=0, keepdims=True)
        whole = whole[:, :channels] + whole[:, channels:]
        sum_ref[:, 0, i * channels : (i + 1) * channels] = jnp.broadcast_to(whole, (sum_ref.shape[0], channels))
    for store in stores:
        store.wait()


def opened_kernel(rows, e_hbm, f_hbm, band_hbm, v_hbm, o_hbm, e_ref, f_ref, band_ref, v_ref, o_ref, sem):
    for load in fetch(sem.at[0], (e_hbm, e_ref), (f_hbm, f_ref), (band_hbm, band_ref), (v_hbm, v_ref)):
        load.wait()
    channels = v_ref.shape[1]
    high = rows + 2
    stores = []
    for first in (0, 2):
        here = pl.ds(first, 2)
        for pair in range(COLS // SEG // 2):
            lhs = windows(e_ref, f_ref, pair, (first, first + 2), (0, high))
            out = jnp.dot(lhs, band_ref[...], preferred_element_type=F32)
            for e in range(2):
                part = out[:, e * channels : (e + 1) * channels] + v_ref[0:1, :]
                o_ref[here, :, 2 * pair + e] = part.reshape(2, high, SEG, channels)
        stores += fetch(sem.at[1 + first // 2], (o_ref.at[here], o_hbm.at[here]))
    for store in stores:
        store.wait()


def second_kernel(
    rows, entries, sum_ref, o_hbm, w_hbm, v_hbm, out_hbm,
    a_ref, place_ref, main_ref, two_ref, one_ref, w_ref, o_ref, v_ref, out_ref, sem,
):
    channels = v_ref.shape[1]
    per = COLS // SEG
    high = rows + 2
    third = 3 * channels
    weights = [
        pltpu.make_async_copy(w_hbm.at[pl.ds(i * third, third)], w_ref.at[pl.ds(i * third, third)], sem.at[i])
        for i in range(9)
    ]
    loads = [pltpu.make_async_copy(o_hbm.at[t], o_ref.at[t], sem.at[9 + t]) for t in range(4)]
    small = pltpu.make_async_copy(v_hbm, v_ref, sem.at[13])
    for copy in (small, loads[0], *weights[:3], loads[1], *weights[3:6], loads[2], *weights[6:], loads[3]):
        copy.start()
    height = lax.axis_index("height")
    frame = lax.axis_index("tm")
    group = channels // GROUPS
    left = jnp.floor((lax.broadcasted_iota(jnp.int32, (channels, channels), 0).astype(F32) + 0.5) / group)
    right = jnp.floor((lax.broadcasted_iota(jnp.int32, (channels, channels), 1).astype(F32) + 0.5) / group)
    same = jnp.where(left == right, 1.0, 0.0).astype(F32)
    total = jnp.sum(sum_ref[:, 0, :], axis=0, keepdims=True)
    both = jnp.concatenate([total[:, :channels], total[:, channels:], jnp.zeros((6, channels), F32)], axis=0)
    totals = jnp.dot(both, same, precision=lax.Precision.HIGHEST, preferred_element_type=F32)
    mean = totals[0:1] / entries
    var = totals[1:2] / entries - mean * mean
    small.wait()
    scale = lax.rsqrt(var + 1e-06) * v_ref[1:2, :]
    half_scale = 0.5 * scale
    half_shift = 0.5 * (v_ref[2:3, :] - mean * scale)
    lane_row = lax.broadcasted_iota(jnp.int32, (SEG, channels), 0)

    def act(t):
        for h in range(high):
            row = height * rows - 1 + h
            inside = (frame * FR_DEV - 2 + t >= 0) & (row >= 0) & (row < rows * lax.axis_size("height"))
            u = o_ref[t, h].reshape(per * SEG, channels) * half_scale + half_shift
            y = u + u * jnp.tanh(u)
            y = jnp.where(inside, y, 0.0)
            a_ref[t, h, 1 : per + 1] = y.astype(BF16).reshape(per, SEG, channels)
            before = jnp.where(lane_row == 0, 0.0, pltpu.roll(y[(per - 1) * SEG :], 1, 0))
            after = jnp.where(lane_row == SEG - 1, 0.0, pltpu.roll(y[:SEG], SEG - 1, 0))
            a_ref[t, h, 0] = before.astype(BF16)
            a_ref[t, h, per + 1] = after.astype(BF16)

    wide = channels // (2 * LANES) * 2 * LANES

    def patch(frame, b, c, count):
        return a_ref[frame, b : b + rows, c : c + count].reshape(rows * count * SEG, channels)

    def tap(a, b, c, lanes):
        row = ((a * 3 + b) * 3 + c) * channels
        return w_ref[row : row + channels, lanes]

    def product(pairs):
        acc = None
        for i in range(0, len(pairs), 2):
            some = pairs[i : i + 2]
            lhs = jnp.concatenate([x() for x, _ in some], axis=1)
            rhs = jnp.concatenate([y() for _, y in some], axis=0)
            part = jnp.dot(lhs, rhs, preferred_element_type=F32)
            acc = part if acc is None else acc + part
        return acc

    def unit(t, a):
        low, rest = slice(0, wide), slice(wide, channels)
        f = t + a
        main = product([
            (functools.partial(patch, f, b, c, per), functools.partial(tap, a, b, c, low))
            for b in range(3) for c in range(3)
        ])
        two = product([
            (
                functools.partial(patch, f, b, 0, per + 1),
                lambda b=b: jnp.concatenate([tap(a, b, 0, rest), tap(a, b, 1, rest)], axis=1),
            )
            for b in range(3)
        ])
        one = product([
            (functools.partial(patch, f, b, 2, per), functools.partial(tap, a, b, 2, rest)) for b in range(3)
        ])
        return main, two, one

    totals_refs = (main_ref, two_ref, one_ref)

    def begin(t):
        for ref, part in zip(totals_refs, unit(t, 0)):
            ref[t] = part

    def add(t, a):
        for ref, part in zip(totals_refs, unit(t, a)):
            ref[t] += part

    def finish(t):
        main, two, one = (ref[t] for ref in totals_refs)
        two = two.reshape(rows, per + 1, SEG, 2 * LANES)
        size = rows * per * SEG
        one = one + two[:, :per, :, :LANES].reshape(size, LANES) + two[:, 1:, :, LANES:].reshape(size, LANES)
        for h in range(rows):
            base = h * per * SEG
            opened = o_ref[t + 2, h + 1].reshape(per * SEG, channels)
            for tile in range(channels // LANES):
                lanes = slice(tile * LANES, (tile + 1) * LANES)
                source = main[:, lanes] if tile * LANES < wide else one
                whole = source[base : base + per * SEG] + v_ref[3:4, lanes] + opened[:, lanes]
                for k in range(per):
                    place_ref[t, h, tile, pl.ds(k, SEG, stride=per), :] = whole[k * SEG : (k + 1) * SEG]
                out_ref[t, h, :, lanes] = place_ref[t, h, tile].astype(BF16)
        store = pltpu.make_async_copy(out_ref.at[t], out_hbm.at[t], sem.at[14 + t])
        store.start()
        return store

    def need(*copies):
        for copy in copies:
            copy.wait()

    need(loads[0])
    act(0)
    need(*weights[:3], loads[1])
    act(1)
    begin(0)
    need(*weights[3:6], loads[2])
    act(2)
    add(0, 1)
    begin(1)
    need(*weights[6:], loads[3])
    act(3)
    add(0, 2)
    add(1, 1)
    first = finish(0)
    add(1, 2)
    second = finish(1)
    need(first, second)


def second_part(rows, entries, sums, opened, weight, vectors):
    high, per, channels, frames = rows + 2, COLS // SEG, vectors.shape[1], FR_DEV
    vmem, hbm = pl.BlockSpec(memory_space=pltpu.VMEM), pl.BlockSpec(memory_space=pltpu.HBM)
    size = rows * per * SEG
    out_shape = (frames, rows, COLS, channels)
    return pl.pallas_call(
        functools.partial(second_kernel, rows, entries),
        out_shape=pltpu.HBM(out_shape, BF16),
        in_specs=[vmem, hbm, hbm, hbm],
        out_specs=hbm,
        scratch_shapes=[
            pltpu.VMEM((4, high, per + 2, SEG, channels), BF16),
            pltpu.VMEM((frames, rows, channels // LANES, COLS, LANES), F32),
            pltpu.VMEM((frames, size, channels // (2 * LANES) * 2 * LANES), F32),
            pltpu.VMEM((frames, size // per * (per + 1), 2 * LANES), F32),
            pltpu.VMEM((frames, size, LANES), F32),
            pltpu.VMEM(weight.shape, BF16),
            pltpu.VMEM(opened.shape, F32),
            pltpu.VMEM(vectors.shape, F32),
            pltpu.VMEM(out_shape, BF16),
            pltpu.SemaphoreType.DMA((16,)),
        ],
        compiler_params=pltpu.CompilerParams(vmem_limit_bytes=36 << 20),
        name="second",
    )(sums, opened, weight, vectors)


def shards(latent, in_weight, in_bias, norm_gain, norm_bias, conv_weight, conv_bias):
    frames = FR_DEV
    rows = latent.shape[0] // frames
    channels = conv_weight.shape[1]
    tm, height = lax.axis_size("tm"), lax.axis_size("height")
    half = height // 2
    core = lax.axis_index("height") % 2
    band, vectors = pl.pallas_call(
        band_kernel,
        out_shape=(
            jax.ShapeDtypeStruct((5 * LANES, 2 * channels), BF16),
            jax.ShapeDtypeStruct((4, channels), F32),
        ),
        name="band",
    )(in_weight, in_bias, norm_gain, norm_bias, conv_bias)

    received = []
    for d in (2, 1, 0):
        route = [
            (i * height + p * half + m, (i + d) * height + 2 * m + p)
            for i in range(tm - d)
            for p in range(2)
            for m in range(half)
        ]
        received.append(lax.ppermute(latent, ("tm", "height"), route))
    own = jnp.stack(received)
    other = lax.ppermute(own, "height", [(i, i ^ 1) for i in range(height)])
    edge = lax.dynamic_slice_in_dim(jnp.stack([own, other]), core * (2 * rows - 2), 2, axis=2)
    swap = [(2 * m - 1, 2 * m) for m in range(1, half)] + [(2 * m, 2 * m - 1) for m in range(1, half)]
    halo = lax.ppermute(edge, "height", swap)

    per = COLS // SEG
    high = rows + 2
    vmem, hbm = pl.BlockSpec(memory_space=pltpu.VMEM), pl.BlockSpec(memory_space=pltpu.HBM)

    def keep(x):
        return pltpu.with_memory_space_constraint(x, pltpu.HBM)

    band, vectors = keep(band), keep(vectors)
    wide_shape, deep_shape = (per // 2, 6, (rows + 4) * SEG, LANES), (per // 2, 4, high * SEG, LANES)
    wide, deep, sums = pl.pallas_call(
        functools.partial(stats_kernel, rows),
        out_shape=(
            pltpu.HBM(wide_shape, BF16),
            pltpu.HBM(deep_shape, BF16),
            jax.ShapeDtypeStruct((tm * height, 1, 2 * channels), F32),
        ),
        in_specs=[vmem, vmem, vmem, hbm, hbm],
        out_specs=(hbm, hbm, vmem),
        scratch_shapes=[
            pltpu.VMEM((2, 6 * 3 * rows * SEG, LANES), F32),
            pltpu.VMEM(band.shape, BF16),
            pltpu.VMEM(vectors.shape, F32),
            pltpu.VMEM(wide_shape, BF16),
            pltpu.VMEM(deep_shape, BF16),
            pltpu.SemaphoreType.DMA((2, 2)),
        ],
        compiler_params=pltpu.CompilerParams(vmem_limit_bytes=12 << 20),
        name="stats",
    )(own, other, halo, band, vectors)
    everyone = [list(range(tm * height))[::-1]]
    sums = lax.all_to_all(sums, ("tm", "height"), 0, 0, tiled=True, axis_index_groups=everyone)
    positions = 4 * high * per * SEG
    opened_shape = (4, high, per, SEG, channels)
    opened = pl.pallas_call(
        functools.partial(opened_kernel, rows),
        out_shape=pltpu.HBM(opened_shape, F32),
        in_specs=[hbm, hbm, hbm, hbm],
        out_specs=hbm,
        scratch_shapes=[
            pltpu.VMEM(wide_shape, BF16),
            pltpu.VMEM(deep_shape, BF16),
            pltpu.VMEM(band.shape, BF16),
            pltpu.VMEM(vectors.shape, F32),
            pltpu.VMEM(opened_shape, F32),
            pltpu.SemaphoreType.DMA((3, 4)),
        ],
        cost_estimate=pl.CostEstimate(
            flops=2 * positions * 5 * LANES * channels, transcendentals=0, bytes_accessed=4 * positions * channels
        ),
        compiler_params=pltpu.CompilerParams(vmem_limit_bytes=16 << 20),
        name="opened",
    )(keep(wide), keep(deep), band, vectors)
    entries = frames * tm * rows * height * COLS * (channels // GROUPS)
    return second_part(rows, entries, sums, keep(opened), keep(conv_weight), vectors)


def solution(mesh):
    return jax.shard_map(
        shards,
        mesh=mesh,
        in_specs=(P(("tm", "height"), None), P(), P(), P(), P(), P(), P()),
        out_specs=P("tm", "height", None, None),
        check_vma=False,
    )
```

time: 64 us -> 51.9 us (0.81)
  waiting for transfers between devices: 14.5 us -> 5.22 us
  local copies, waits for them, and re-layouts: 5.53 us -> 0 us
  Pallas kernels: 21.3 us -> 24.9 us
  starting transfers between devices: 22.1 us -> 21.1 us
    ppermute x5 -> x0, waiting for transfers between devices: 13 us -> none  [pairwise_sum(): x = x + lax.ppermute(x, axis, [(i, i ^ step) for i in range(size)])]
    all_to_all x0 -> x1, starting transfers between devices: none -> 8.62 us  [shards(): lax.all_to_all(sums, ('tm', 'height'), 0, 0, tiled=True, axis_index_group...]
    unnamed x12 -> x0, local copies, waits for them, and re-layouts: 5.52 us -> none
    ppermute x5 -> x0, starting transfers between devices: 4.94 us -> none  [pairwise_sum(): x = x + lax.ppermute(x, axis, [(i, i ^ step) for i in range(size)])]
    ppermute x1, starting transfers between devices: 6.66 us -> 2.14 us  [shards(): other = lax.ppermute(own, 'height', [(i, i ^ 1) for i in range(height)])]
    pallas_call x3 -> x4, Pallas kernels: 21.3 us -> 24.9 us  [the longest x1 14.2 us: second_part(): pl.pallas_call(functools.partial(second_kernel, rows, entries), out_shape...]
    all_to_all x0 -> x1, waiting for transfers between devices: none -> 2.29 us  [shards(): lax.all_to_all(sums, ('tm', 'height'), 0, 0, tiled=True, axis_index_group...]
    ppermute x3, waiting for transfers between devices: 0.54 us -> 1.95 us  [shards(): received.append(lax.ppermute(latent, ('tm', 'height'), route))]
  transfers between devices with their start and end apart: 10 -> 6, of which waited for: 7 -> 3; matrix products, arithmetic and copies ran while one was open for 0% -> 0% of each run, Pallas kernels for 5% -> 14%
where the time goes in v1:
time: 51.9 us; the launch traced here: 51.6 us
  Pallas kernels  24.9 us (48%)
  starting transfers between devices  21.1 us (41%)
  waiting for transfers between devices  5.22 us (10%)
    pallas_call x1, Pallas kernels, second_part(): pl.pallas_call(functools.partial(second_kernel, rows, entries), out_shape...  14.2 us
    ppermute x3, starting transfers between devices, shards(): received.append(lax.ppermute(latent, ('tm', 'height'), route))  9.71 us
    all_to_all x1, starting transfers between devices, shards(): lax.all_to_all(sums, ('tm', 'height'), 0, 0, tiled=True, axis_index_group...  8.62 us
    pallas_call x1, Pallas kernels, shards(): pl.pallas_call(functools.partial(opened_kernel, rows), out_shape=pltpu.HB...  5.24 us
    pallas_call x1, Pallas kernels, shards(): pl.pallas_call(functools.partial(stats_kernel, rows), out_shape=(pltpu.HB...  3.39 us
    all_to_all x1, waiting for transfers between devices, shards(): lax.all_to_all(sums, ('tm', 'height'), 0, 0, tiled=True, axis_index_group...  2.29 us
    ppermute x1, starting transfers between devices, shards(): other = lax.ppermute(own, 'height', [(i, i ^ 1) for i in range(height)])  2.14 us
    pallas_call x1, Pallas kernels, shards(): pl.pallas_call(band_kernel, out_shape=(jax.ShapeDtypeStruct((5 * LANES, 2...  2.1 us
  transfers between devices with their start and end apart: 6, of which 3 were waited for; matrix products, arithmetic and copies ran while one was open for 0% of the time, Pallas kernels for 14%

profile of v1, /device:TPU:0, one launch (start us, length us, event | category | flops | bytes accessed | tf_op | source)
XLA Modules:
  0.0 51.6 jit_solution(5938916661584060336)
XLA Ops:
  0.0 4.9 %collective-permute-start = (bf16[6,2560]{1,0:T(8,128)(2,1)}, bf16[6,2560]{1,0:T(8,128)(2,1)S(1)}, u32[]{:S(2)}, u32[]{:S(2)}) collective-permute-start(bf16[6,2560]{1,0:T(8,128)(2,1)} %param.7), channel_id=1, source_target_pairs={{0,16},{1,18},{2,20},{3,22},{4,17},{5,19},{6,21},{7,23},{8,24},{9,... | collective-permute-start | bytes 92168 | tf_op jit(solution)/shard_map/ppermute | solution.py:337
  4.9 1.4 %collective-permute-start.2 = (bf16[6,2560]{1,0:T(8,128)(2,1)}, bf16[6,2560]{1,0:T(8,128)(2,1)S(1)}, u32[]{:S(2)}, u32[]{:S(2)}) collective-permute-start(bf16[6,2560]{1,0:T(8,128)(2,1)} %param.7), channel_id=1, source_target_pairs={{0,0},{1,2},{2,4},{3,6},{4,1},{5,3},{6,5},{7,7},{8,8},{9,10},{10,1... | collective-permute-start | bytes 92168 | tf_op jit(solution)/shard_map/ppermute | solution.py:337
  6.3 3.4 %collective-permute-start.1 = (bf16[6,2560]{1,0:T(8,128)(2,1)}, bf16[6,2560]{1,0:T(8,128)(2,1)S(1)}, u32[]{:S(2)}, u32[]{:S(2)}) collective-permute-start(bf16[6,2560]{1,0:T(8,128)(2,1)} %param.7), channel_id=1, source_target_pairs={{0,8},{1,10},{2,12},{3,14},{4,9},{5,11},{6,13},{7,15},{8,16},{9,18... | collective-permute-start | bytes 92168 | tf_op jit(solution)/shard_map/ppermute | solution.py:337
  9.7 0.0 collective-permute-done
  9.7 0.0 collective-permute-done.2
  9.7 1.9 %collective-permute-done.1 = bf16[6,2560]{1,0:T(8,128)(2,1)S(1)} collective-permute-done((bf16[6,2560]{1,0:T(8,128)(2,1)}, bf16[6,2560]{1,0:T(8,128)(2,1)S(1)}, u32[]{:S(2)}, u32[]{:S(2)}) %collective-permute-start.1) | collective-permute-done | bytes 30752 | tf_op jit(solution)/shard_map/ppermute | solution.py:337
  11.7 2.1 %collective-permute-start.3 = (bf16[3,6,2560]{2,1,0:T(8,128)(2,1)S(1)}, bf16[3,6,2560]{2,1,0:T(8,128)(2,1)S(1)}, u32[]{:S(2)}, u32[]{:S(2)}) collective-permute-start(bf16[3,6,2560]{2,1,0:T(8,128)(2,1)S(1)} %get-tuple-element.16.own_ref), channel_id=1, source_target_pairs={{0,1},{1,0},{2,3},{3,2},{4,5},{5,4},{6,7},{7,6},{8,9},{9,8},{10,11... | collective-permute-start | bytes 276488 | tf_op jit(solution)/shard_map/ppermute | solution.py:339
  13.9 1.0 %collective-permute-done.3.other_ref = bf16[3,6,2560]{2,1,0:T(8,128)(2,1)S(1)} collective-permute-done((bf16[3,6,2560]{2,1,0:T(8,128)(2,1)S(1)}, bf16[3,6,2560]{2,1,0:T(8,128)(2,1)S(1)}, u32[]{:S(2)}, u32[]{:S(2)}) %collective-permute-start.3) | collective-permute-done | bytes 92192 | tf_op jit(solution)/shard_map/ppermute | solution.py:339
  14.8 0.1 fusion
  14.9 0.7 %collective-permute-start.4 = (bf16[2,3,2,2560]{3,2,1,0:T(2,128)(2,1)S(1)}, bf16[2,3,2,2560]{3,2,1,0:T(2,128)(2,1)S(1)}, u32[]{:S(2)}, u32[]{:S(2)}) collective-permute-start(bf16[2,3,2,2560]{3,2,1,0:T(2,128)(2,1)S(1)} %fusion), channel_id=1, source_target_pairs={{1,2},{3,4},{5,6},{2,1},{4,3},{6,5},{9,10},{11,12},{13,14},{10,9},... | collective-permute-start | bytes 184328 | tf_op jit(solution)/shard_map/ppermute | solution.py:342
  15.6 2.1 %band.1 = (bf16[640,768]{1,0:T(8,128)(2,1)}, f32[4,384]{1,0:T(4,128)}) custom-call(bf16[432,384]{1,0:T(8,128)(2,1)} %w_ref.1, f32[384]{0:T(512)} %refs_0_.1, f32[384]{0:T(512)} %refs_1_.1, f32[384]{0:T(512)} %refs_2_.1, f32[384]{0:T(512)} %refs_3_.1), custom_call_target="tpu_custom_call" | custom-call | tf_op jit(solution)/shard_map/band/pallas_call | solution.py:320
  17.7 0.0 collective-permute-done.4.halo_ref
  17.7 3.4 %stats.1 = (bf16[5,6,112,128]{3,2,1,0:T(8,128)(2,1)}, bf16[5,4,80,128]{3,2,1,0:T(8,128)(2,1)}, f32[32,1,768]{2,1,0:T(1,128)}) custom-call(bf16[3,6,2560]{2,1,0:T(8,128)(2,1)S(1)} %get-tuple-element.16.own_ref, bf16[3,6,2560]{2,1,0:T(8,128)(2,1)S(1)} %collective-permute-done.3.other_ref, bf16[2,3,2,2560]{3,2,1,0:T(2,128)(2,1)S(1)} %collective-permute-done.4.halo_ref, ...), custom_call_target="tpu_custom_call" | custom-call | tf_op jit(solution)/shard_map/stats/pallas_call | solution.py:353
  21.1 8.6 %all-to-all-start = ((f32[32,1,768]{2,1,0:T(1,128)}), f32[32,1,768]{2,1,0:T(1,128)S(1)}, u32[]{:S(2)}, u32[]{:S(2)}) async-start(f32[32,1,768]{2,1,0:T(1,128)} %get-tuple-element.12), calls=%async_computation | async-start | bytes 196608 | tf_op jit(solution)/shard_map/all_to_all | solution.py:374
  29.7 5.2 %opened.1.o_hbm = f32[4,5,10,16,384]{4,3,2,1,0:T(8,128)} custom-call(bf16[5,6,112,128]{3,2,1,0:T(8,128)(2,1)} %get-tuple-element.13.e_hbm, bf16[5,4,80,128]{3,2,1,0:T(8,128)(2,1)} %get-tuple-element.14.f_hbm, bf16[640,768]{1,0:T(8,128)(2,1)} %get-tuple-element.10.band_hbm, f32[4,384]{1,0:T(4,128)} %get-tuple-element.11.v_hbm), custom_call_target="tpu_custom_call" | custom-call | flops 1572864000 | bytes 4915200 | tf_op jit(solution)/shard_map/opened/pallas_call | solution.py:377
  35.0 2.3 %all-to-all-done.sum_ref = f32[32,1,768]{2,1,0:T(1,128)S(1)} async-done(((f32[32,1,768]{2,1,0:T(1,128)}), f32[32,1,768]{2,1,0:T(1,128)S(1)}, u32[]{:S(2)}, u32[]{:S(2)}) %all-to-all-start) | async-done | bytes 98336 | tf_op jit(solution)/shard_map/all_to_all | solution.py:374
  37.3 14.2 %second.1 = bf16[2,3,160,384]{3,2,1,0:T(8,128)(2,1)} custom-call(f32[32,1,768]{2,1,0:T(1,128)S(1)} %all-to-all-done.sum_ref, f32[4,5,10,16,384]{4,3,2,1,0:T(8,128)} %opened.1.o_hbm, bf16[10368,384]{1,0:T(8,128)(2,1)} %w_hbm.1, f32[4,384]{1,0:T(4,128)} %get-tuple-element.11.v_hbm), custom_call_target="tpu_custom_call" | custom-call | tf_op jit(solution)/shard_map/second/pallas_call | solution.py:291
  (1 shorter events, 0.0 us)
Async XLA Ops:
  0.0 9.7 %collective-permute-start = (bf16[6,2560]{1,0:T(8,128)(2,1)}, bf16[6,2560]{1,0:T(8,128)(2,1)S(1)}, u32[]{:S(2)}, u32[]{:S(2)}) collective-permute-start(bf16[6,2560]{1,0:T(8,128)(2,1)} %param.7), channel_id=1, source_target_pairs={{0,16},{1,18},{2,20},{3,22},{4,17},{5,19},{6,21},{7,23},{8,24},{9,... | collective-permute-start | bytes 92168 | tf_op jit(solution)/shard_map/ppermute | solution.py:337
  4.9 4.8 %collective-permute-start.2 = (bf16[6,2560]{1,0:T(8,128)(2,1)}, bf16[6,2560]{1,0:T(8,128)(2,1)S(1)}, u32[]{:S(2)}, u32[]{:S(2)}) collective-permute-start(bf16[6,2560]{1,0:T(8,128)(2,1)} %param.7), channel_id=1, source_target_pairs={{0,0},{1,2},{2,4},{3,6},{4,1},{5,3},{6,5},{7,7},{8,8},{9,10},{10,1... | collective-permute-start | bytes 92168 | tf_op jit(solution)/shard_map/ppermute | solution.py:337
  6.3 5.4 %collective-permute-start.1 = (bf16[6,2560]{1,0:T(8,128)(2,1)}, bf16[6,2560]{1,0:T(8,128)(2,1)S(1)}, u32[]{:S(2)}, u32[]{:S(2)}) collective-permute-start(bf16[6,2560]{1,0:T(8,128)(2,1)} %param.7), channel_id=1, source_target_pairs={{0,8},{1,10},{2,12},{3,14},{4,9},{5,11},{6,13},{7,15},{8,16},{9,18... | collective-permute-start | bytes 92168 | tf_op jit(solution)/shard_map/ppermute | solution.py:337
  11.7 3.1 %collective-permute-start.3 = (bf16[3,6,2560]{2,1,0:T(8,128)(2,1)S(1)}, bf16[3,6,2560]{2,1,0:T(8,128)(2,1)S(1)}, u32[]{:S(2)}, u32[]{:S(2)}) collective-permute-start(bf16[3,6,2560]{2,1,0:T(8,128)(2,1)S(1)} %get-tuple-element.16.own_ref), channel_id=1, source_target_pairs={{0,1},{1,0},{2,3},{3,2},{4,5},{5,4},{6,7},{7,6},{8,9},{9,8},{10,11... | collective-permute-start | bytes 276488 | tf_op jit(solution)/shard_map/ppermute | solution.py:339
  14.9 2.8 %collective-permute-start.4 = (bf16[2,3,2,2560]{3,2,1,0:T(2,128)(2,1)S(1)}, bf16[2,3,2,2560]{3,2,1,0:T(2,128)(2,1)S(1)}, u32[]{:S(2)}, u32[]{:S(2)}) collective-permute-start(bf16[2,3,2,2560]{3,2,1,0:T(2,128)(2,1)S(1)} %fusion), channel_id=1, source_target_pairs={{1,2},{3,4},{5,6},{2,1},{4,3},{6,5},{9,10},{11,12},{13,14},{10,9},... | collective-permute-start | bytes 184328 | tf_op jit(solution)/shard_map/ppermute | solution.py:342
  21.1 16.2 %all-to-all-start = ((f32[32,1,768]{2,1,0:T(1,128)}), f32[32,1,768]{2,1,0:T(1,128)S(1)}, u32[]{:S(2)}, u32[]{:S(2)}) async-start(f32[32,1,768]{2,1,0:T(1,128)} %get-tuple-element.12), calls=%async_computation | async-start | bytes 196608 | tf_op jit(solution)/shard_map/all_to_all | solution.py:374

commit v2 on v1

v2 whole, which is shorter than its diff:
```python
import functools

import jax
import jax.numpy as jnp
from jax import lax
from jax.experimental import pallas as pl
from jax.experimental.pallas import tpu as pltpu
from jax.sharding import PartitionSpec as P

C_IN = 16
GROUPS = 32
COLS = 160
FR_DEV = 2
SEG = 16
LANES = 128
F32 = jnp.float32
BF16 = jnp.bfloat16


def band_kernel(w_ref, *refs):
    *vectors, o_ref, v_ref = refs
    for i, vector in enumerate(vectors):
        v_ref[i : i + 1, :] = vector[...].reshape(1, -1)
    o_ref[...] = jnp.zeros_like(o_ref)
    channels = w_ref.shape[1]
    depth = 3 * C_IN
    places = [(a, b, a, b) for a in range(3) for b in range(2)] + [(0, 2, 3, 0), (1, 2, 3, 1), (2, 2, 4, 0)]
    for a, b, group, side in places:
        for e in range(2):
            row = group * LANES + side * (LANES // 2) + e * C_IN
            tap = (a * 3 + b) * depth
            o_ref[row : row + depth, e * channels : (e + 1) * channels] = w_ref[tap : tap + depth, :]


def windows(e_ref, f_ref, pair, frames, high):
    (t0, t1), (h0, h1) = frames, high
    rows = slice(h0 * SEG, h1 * SEG)
    parts = [e_ref[pair, t0 + a : t1 + a, rows] for a in range(3)]
    parts.append(f_ref[pair, t0:t1, rows])
    parts.append(e_ref[pair, t0 + 2 : t1 + 2, (h0 + 2) * SEG : (h1 + 2) * SEG])
    size = (t1 - t0) * (h1 - h0) * SEG
    return jnp.concatenate([part.reshape(size, LANES) for part in parts], axis=1)


def fetch(sem, *pairs):
    copies = [pltpu.make_async_copy(source, target, sem.at[i]) for i, (source, target) in enumerate(pairs)]
    for copy in copies:
        copy.start()
    return copies


def lay_out(rows, own_ref, other_ref, halo_ref, z_ref, e_ref, f_ref):
    core = lax.rem(lax.axis_index("height"), 2)
    slots = 3 * rows
    per = COLS // SEG
    high = rows + 2

    for frame in range(6):
        for slot in (0, slots - 1):
            row = (frame * slots + slot) * SEG
            for half in range(2):
                z_ref[half, row : row + SEG, :] = jnp.zeros((SEG, LANES), F32)

    def spread(piece, frame, slot):
        base = pl.multiple_of((frame * slots + slot) * SEG, SEG)
        count = piece.shape[0]
        edge = jnp.zeros((count, LANES), F32)
        wide = jnp.concatenate([edge, piece, edge, edge], axis=1)
        for s in range(SEG):
            for half in range(2):
                start = LANES + s * per * C_IN - C_IN + half * 6 * C_IN
                lo = start // LANES * LANES
                window = wide[:, lo : lo + 2 * LANES]
                if start > lo:
                    window = pltpu.roll(window, 2 * LANES - (start - lo), 1)
                z_ref[half, pl.ds(base + s, count, stride=SEG), :] = window[:, :LANES]

    main = jnp.where(core == 0, rows, 0)
    edge_slot = jnp.where(core == 0, rows - 2, 2 * rows)
    for d in range(3):
        real = lax.axis_index("tm") >= 2 - d

        def piece(ref, *index):
            x = ref[(*index, d)].astype(F32)
            return x if d == 2 else jnp.where(real, x, 0.0)

        spread(piece(own_ref), 2 * d + core, main)
        spread(piece(other_ref), 2 * d + 1 - core, main)
        spread(piece(halo_ref, 0), 2 * d + 1 - core, edge_slot)
        spread(piece(halo_ref, 1), 2 * d + core, edge_slot)

    first = rows - 2
    span = rows + 4
    low_side = lax.broadcasted_iota(jnp.int32, (span * SEG, LANES), 1) < LANES // 2
    where = [(0, 0), (0, 2 * C_IN), (0, 4 * C_IN), (1, 0), (1, 2 * C_IN)]

    def turned(x, shift):
        return x if shift % LANES == 0 else pltpu.roll(x, shift % LANES, 1)

    for pair, (half, offset) in enumerate(where):
        upper = []
        for frame in range(6):
            x = z_ref[half, pl.ds((frame * slots + first) * SEG, (span + 1) * SEG), :]
            low, up = turned(x, -offset), turned(x, LANES // 2 - offset)
            e_ref[pair, frame] = jnp.where(low_side, low[: span * SEG], up[SEG:]).astype(BF16)
            if 0 < frame < 5:
                f_ref[pair, frame - 1] = jnp.where(
                    low_side[: high * SEG], upper, up[2 * SEG : span * SEG]
                ).astype(BF16)
            upper = low[2 * SEG : span * SEG]


def stats_kernel(rows, own_ref, other_ref, halo_ref, band_ref, v_ref, sum_ref, z_ref, e_ref, f_ref):
    lay_out(rows, own_ref, other_ref, halo_ref, z_ref, e_ref, f_ref)
    channels = v_ref.shape[1]
    per = COLS // SEG
    sums = jnp.zeros((8, 2 * channels), F32)
    squares = jnp.zeros((8, 2 * channels), F32)
    bias = jnp.concatenate([v_ref[0:1, :], v_ref[0:1, :]], axis=1)
    for pair in range(per // 2):
        out = jnp.dot(
            windows(e_ref, f_ref, pair, (2, 4), (1, 1 + rows)), band_ref[...], preferred_element_type=F32
        )
        out = (out + bias).reshape(-1, 8, 2 * channels)
        sums = sums + jnp.sum(out, axis=0)
        squares = squares + jnp.sum(out * out, axis=0)
    for i, part in enumerate((sums, squares)):
        whole = jnp.sum(part, axis=0, keepdims=True)
        whole = whole[:, :channels] + whole[:, channels:]
        sum_ref[:, 0, i * channels : (i + 1) * channels] = jnp.broadcast_to(whole, (sum_ref.shape[0], channels))


def opened_kernel(
    rows, own_ref, other_ref, halo_ref, band_ref, v_ref, first_ref, o_hbm, z_ref, e_ref, f_ref, o_ref, sem
):
    lay_out(rows, own_ref, other_ref, halo_ref, z_ref, e_ref, f_ref)
    channels = v_ref.shape[1]
    high = rows + 2
    stores = []
    for t0, t1 in ((2, 4), (1, 2), (0, 1)):
        here = pl.ds(t0 - 1, t1 - t0)
        for pair in range(COLS // SEG // 2):
            lhs = windows(e_ref, f_ref, pair, (t0, t1), (0, high))
            out = jnp.dot(lhs, band_ref[...], preferred_element_type=F32)
            for e in range(2):
                part = out[:, e * channels : (e + 1) * channels] + v_ref[0:1, :]
                part = part.reshape(t1 - t0, high, SEG, channels)
                if t0:
                    o_ref[here, :, 2 * pair + e] = part
                else:
                    first_ref[:, 2 * pair + e] = part[0]
        if t0:
            stores += fetch(sem.at[t0 - 1], (o_ref.at[here], o_hbm.at[here]))
    for store in stores:
        store.wait()


def second_kernel(
    rows, entries, sum_ref, first_ref, o_hbm, head_ref, w_hbm, v_ref, out_hbm,
    a_ref, place_ref, main_ref, two_ref, w_ref, o_ref, out_ref, sem,
):
    channels = v_ref.shape[1]
    per = COLS // SEG
    high = rows + 2
    third = 3 * channels
    weights = [
        pltpu.make_async_copy(w_hbm.at[pl.ds(i * third, third)], w_ref.at[pl.ds((i - 2) * third, third)], sem.at[i])
        for i in range(2, 9)
    ]
    loads = [pltpu.make_async_copy(o_hbm.at[t], o_ref.at[t], sem.at[9 + t]) for t in range(3)]
    for copy in (loads[0], *weights[:4], loads[1], *weights[4:], loads[2]):
        copy.start()
    height = lax.axis_index("height")
    frame = lax.axis_index("tm")
    group = channels // GROUPS
    left = jnp.floor((lax.broadcasted_iota(jnp.int32, (channels, channels), 0).astype(F32) + 0.5) / group)
    right = jnp.floor((lax.broadcasted_iota(jnp.int32, (channels, channels), 1).astype(F32) + 0.5) / group)
    same = jnp.where(left == right, 1.0, 0.0).astype(F32)
    total = jnp.sum(sum_ref[:, 0, :], axis=0, keepdims=True)
    both = jnp.concatenate([total[:, :channels], total[:, channels:], jnp.zeros((6, channels), F32)], axis=0)
    totals = jnp.dot(both, same, precision=lax.Precision.HIGHEST, preferred_element_type=F32)
    mean = totals[0:1] / entries
    var = totals[1:2] / entries - mean * mean
    scale = lax.rsqrt(var + 1e-06) * v_ref[1:2, :]
    half_scale = 0.5 * scale
    half_shift = 0.5 * (v_ref[2:3, :] - mean * scale)
    lane_row = lax.broadcasted_iota(jnp.int32, (SEG, channels), 0)

    def act_rows(t):
        return [functools.partial(act, t, h) for h in range(high)]

    def act(t, *hs):
        for h in hs or range(high):
            row = height * rows - 1 + h
            inside = (frame * FR_DEV - 2 + t >= 0) & (row >= 0) & (row < rows * lax.axis_size("height"))
            x = o_ref[t - 1, h] if t else first_ref[h]
            u = x.reshape(per * SEG, channels) * half_scale + half_shift
            y = u + u * jnp.tanh(u)
            y = jnp.where(inside, y, 0.0)
            a_ref[t, h, 1 : per + 1] = y.astype(BF16).reshape(per, SEG, channels)
            before = jnp.where(lane_row == 0, 0.0, pltpu.roll(y[(per - 1) * SEG :], 1, 0))
            after = jnp.where(lane_row == SEG - 1, 0.0, pltpu.roll(y[:SEG], SEG - 1, 0))
            a_ref[t, h, 0] = before.astype(BF16)
            a_ref[t, h, per + 1] = after.astype(BF16)

    wide = channels // (2 * LANES) * 2 * LANES

    def patch(frame, b, c, count):
        return a_ref[frame, b : b + rows, c : c + count].reshape(rows * count * SEG, channels)

    def tap(a, b, c, lanes):
        row = ((a * 3 + b) * 3 + c) * channels
        if row < head_ref.shape[0]:
            return head_ref[row : row + channels, lanes]
        row -= head_ref.shape[0]
        return w_ref[row : row + channels, lanes]

    def product(pairs, beside=()):
        beside = list(beside)
        acc = None
        for i in range(0, len(pairs), 2):
            some = pairs[i : i + 2]
            lhs = jnp.concatenate([x() for x, _ in some], axis=1)
            rhs = jnp.concatenate([y() for _, y in some], axis=0)
            part = jnp.dot(lhs, rhs, preferred_element_type=F32)
            acc = part if acc is None else acc + part
            if beside:
                beside.pop(0)()
        for step in beside:
            step()
        return acc

    low, rest = slice(0, wide), slice(wide, channels)

    def edge(t, a, start):
        f = t + a
        for i, (bs, beside) in enumerate(start):
            parts = (
                product([
                    (functools.partial(patch, f, b, c, per), functools.partial(tap, a, b, c, low))
                    for b in bs for c in range(3)
                ], beside),
                product([
                    (
                        functools.partial(patch, f, b, 0, per + 1),
                        lambda b=b: jnp.concatenate([tap(a, b, 0, rest), tap(a, b, 1, rest)], axis=1),
                    )
                    for b in bs
                ]),
                product([
                    (functools.partial(patch, f, b, 2, per), functools.partial(tap, a, b, 2, rest)) for b in bs
                ]),
            )
            if i == 0 and a == 0:
                main_ref[t, :, low], two_ref[t], main_ref[t, :, rest] = parts
            elif i == 0:
                two_ref[t] = parts[1]
                main_ref[t, :, low] += parts[0]
                main_ref[t, :, rest] += parts[2]
            else:
                two_ref[t] += parts[1]
                main_ref[t, :, low] += parts[0]
                main_ref[t, :, rest] += parts[2]

    def shared(f, beside):
        whole = slice(0, channels)
        both = product([
            (
                functools.partial(patch, f, b, c, per),
                lambda b=b, c=c: jnp.concatenate([tap(f, b, c, whole), tap(f - 1, b, c, whole)], axis=1),
            )
            for b in range(3) for c in range(3)
        ], beside)
        main_ref[0] += both[:, :channels]
        if f == 1:
            main_ref[1] = both[:, channels:]
        else:
            main_ref[1] += both[:, channels:]

    def finish(t):
        two = two_ref[t].reshape(rows, per + 1, SEG, 2 * LANES)
        size = rows * per * SEG
        main = main_ref[t, :, low]
        one = main_ref[t, :, rest]
        one = one + two[:, :per, :, :LANES].reshape(size, LANES) + two[:, 1:, :, LANES:].reshape(size, LANES)
        for h in range(rows):
            base = h * per * SEG
            opened = o_ref[t + 1, h + 1].reshape(per * SEG, channels)
            for tile in range(channels // LANES):
                lanes = slice(tile * LANES, (tile + 1) * LANES)
                source = main[:, lanes] if tile * LANES < wide else one
                whole = source[base : base + per * SEG] + v_ref[3:4, lanes] + opened[:, lanes]
                for k in range(per):
                    place_ref[t, h, tile, pl.ds(k, SEG, stride=per), :] = whole[k * SEG : (k + 1) * SEG]
                out_ref[t, h, :, lanes] = place_ref[t, h, tile].astype(BF16)
        store = pltpu.make_async_copy(out_ref.at[t], out_hbm.at[t], sem.at[14 + t])
        store.start()
        return store

    def need(*copies):
        for copy in copies:
            copy.wait()

    def steps(*parts):
        return [lambda group=group: [step() for step in group] for group in parts]

    rows1, rows2, rows3 = (act_rows(t) for t in (1, 2, 3))
    act(0)
    wait1 = functools.partial(need, weights[0], loads[0])
    wait2 = functools.partial(need, *weights[1:4], loads[1])
    wait3 = functools.partial(need, *weights[4:], loads[2])
    edge(0, 0, [((0, 1), steps([], [wait1])), ((2,), steps(rows1, [wait2]))])
    shared(1, steps(rows2, [wait3]))
    shared(2, steps(rows3))
    first = finish(0)
    edge(1, 2, [((0, 1, 2), [])])
    second = finish(1)
    need(first, second)


def second_part(rows, entries, sums, first, opened, head, weight, vectors):
    high, per, channels, frames = rows + 2, COLS // SEG, vectors.shape[1], FR_DEV
    vmem, hbm = pl.BlockSpec(memory_space=pltpu.VMEM), pl.BlockSpec(memory_space=pltpu.HBM)
    size = rows * per * SEG
    out_shape = (frames, rows, COLS, channels)
    return pl.pallas_call(
        functools.partial(second_kernel, rows, entries),
        out_shape=pltpu.HBM(out_shape, BF16),
        in_specs=[vmem, vmem, hbm, vmem, hbm, vmem],
        out_specs=hbm,
        scratch_shapes=[
            pltpu.VMEM((4, high, per + 2, SEG, channels), BF16),
            pltpu.VMEM((frames, rows, channels // LANES, COLS, LANES), F32),
            pltpu.VMEM((frames, size, channels), F32),
            pltpu.VMEM((frames, size // per * (per + 1), 2 * LANES), F32),
            pltpu.VMEM((weight.shape[0] - head.shape[0], channels), BF16),
            pltpu.VMEM(opened.shape, F32),
            pltpu.VMEM(out_shape, BF16),
            pltpu.SemaphoreType.DMA((16,)),
        ],
        compiler_params=pltpu.CompilerParams(vmem_limit_bytes=36 << 20),
        name="second",
    )(sums, first, opened, head, weight, vectors)


def shards(latent, in_weight, in_bias, norm_gain, norm_bias, conv_weight, conv_bias):
    frames = FR_DEV
    rows = latent.shape[0] // frames
    channels = conv_weight.shape[1]
    tm, height = lax.axis_size("tm"), lax.axis_size("height")
    half = height // 2
    core = lax.axis_index("height") % 2
    band, vectors = pl.pallas_call(
        band_kernel,
        out_shape=(
            pltpu.VMEM((5 * LANES, 2 * channels), BF16),
            pltpu.VMEM((4, channels), F32),
        ),
        name="band",
    )(in_weight, in_bias, norm_gain, norm_bias, conv_bias)

    received = []
    for d in (2, 1, 0):
        route = [
            (i * height + p * half + m, (i + d) % tm * height + 2 * m + p)
            for i in range(tm)
            for p in range(2)
            for m in range(half)
        ]
        received.append(lax.ppermute(latent, ("tm", "height"), route))
    own = jnp.stack(received)
    other = lax.ppermute(own, "height", [(i, i ^ 1) for i in range(height)])
    edge = lax.dynamic_slice_in_dim(jnp.stack([own, other]), core * (2 * rows - 2), 2, axis=2)
    swap = [(2 * m - 1, 2 * m) for m in range(1, half)] + [(2 * m, 2 * m - 1) for m in range(1, half)]
    halo = lax.ppermute(edge, "height", swap)

    per = COLS // SEG
    high = rows + 2
    vmem, hbm = pl.BlockSpec(memory_space=pltpu.VMEM), pl.BlockSpec(memory_space=pltpu.HBM)

    def keep(x):
        return pltpu.with_memory_space_constraint(x, pltpu.HBM)

    scratch = [
        pltpu.VMEM((2, 6 * 3 * rows * SEG, LANES), F32),
        pltpu.VMEM((per // 2, 6, (rows + 4) * SEG, LANES), BF16),
        pltpu.VMEM((per // 2, 4, high * SEG, LANES), BF16),
    ]
    sums = pl.pallas_call(
        functools.partial(stats_kernel, rows),
        out_shape=jax.ShapeDtypeStruct((tm * height, 1, 2 * channels), F32),
        in_specs=[vmem] * 5,
        scratch_shapes=scratch,
        compiler_params=pltpu.CompilerParams(vmem_limit_bytes=12 << 20),
        name="stats",
    )(own, other, halo, band, vectors)
    sums = lax.all_to_all(sums, ("tm", "height"), 0, 0, tiled=True)
    positions = 4 * high * per * SEG
    opened_shape = (3, high, per, SEG, channels)
    first, opened = pl.pallas_call(
        functools.partial(opened_kernel, rows),
        out_shape=(pltpu.VMEM(opened_shape[1:], F32), pltpu.HBM(opened_shape, F32)),
        in_specs=[vmem] * 5,
        out_specs=(vmem, hbm),
        scratch_shapes=[*scratch, pltpu.VMEM(opened_shape, F32), pltpu.SemaphoreType.DMA((2, 1))],
        cost_estimate=pl.CostEstimate(
            flops=2 * positions * 5 * LANES * channels, transcendentals=0, bytes_accessed=4 * positions * channels
        ),
        compiler_params=pltpu.CompilerParams(vmem_limit_bytes=16 << 20),
        name="opened",
    )(own, other, halo, band, vectors)
    entries = frames * tm * rows * height * COLS * (channels // GROUPS)
    head = pltpu.with_memory_space_constraint(conv_weight[: 6 * channels], pltpu.VMEM)
    return second_part(rows, entries, sums, first, keep(opened), head, keep(conv_weight), vectors)


def solution(mesh):
    return jax.shard_map(
        shards,
        mesh=mesh,
        in_specs=(P(("tm", "height"), None), P(), P(), P(), P(), P(), P()),
        out_specs=P("tm", "height", None, None),
        check_vma=False,
    )
```

time: 51.9 us -> 45.1 us (0.87)
  Pallas kernels: 24.9 us -> 19.4 us
  starting transfers between devices: 21.1 us -> 18 us
  local copies, waits for them, and re-layouts: 0 us -> 2.86 us
  waiting for transfers between devices: 5.22 us -> 4.22 us
    ppermute x3, starting transfers between devices: 9.71 us -> 5.91 us  [shards(): received.append(lax.ppermute(latent, ('tm', 'height'), route))]
    pallas_call x3, Pallas kernels: 10.7 us -> 7.07 us  [the longest x1 3.65 us: shards(): pl.pallas_call(functools.partial(opened_kernel, rows), out_shape=(pltpu.V...]
    ppermute x1, starting transfers between devices: 2.14 us -> 5 us  [shards(): other = lax.ppermute(own, 'height', [(i, i ^ 1) for i in range(height)])]
    all_to_all x1, starting transfers between devices: 8.62 us -> 6.43 us  [shards(): sums = lax.all_to_all(sums, ('tm', 'height'), 0, 0, tiled=True)]
    pallas_call x1, Pallas kernels: 14.2 us -> 12.3 us  [second_part(): pl.pallas_call(functools.partial(second_kernel, rows, entries), out_shape...]
    slice x0 -> x1, local copies, waits for them, and re-layouts: none -> 1.66 us  [shards(): conv_weight[:6 * channels]]
    all_to_all x1, waiting for transfers between devices: 2.29 us -> 1.05 us  [shards(): sums = lax.all_to_all(sums, ('tm', 'height'), 0, 0, tiled=True)]
    unnamed x0 -> x4, local copies, waits for them, and re-layouts: none -> 1.2 us
  transfers between devices with their start and end apart: 6 -> 6, of which waited for: 3 -> 3; matrix products, arithmetic and copies ran while one was open for 0% -> 4% of each run, Pallas kernels for 14% -> 11%
where the time goes in v2:
time: 45.1 us; the launch traced here: 44.8 us
  Pallas kernels  19.4 us (43%)
  starting transfers between devices  18 us (40%)
  waiting for transfers between devices  4.22 us (9%)
  local copies, waits for them, and re-layouts  2.86 us (6%)
    pallas_call x1, Pallas kernels, second_part(): pl.pallas_call(functools.partial(second_kernel, rows, entries), out_shape...  12.3 us
    all_to_all x1, starting transfers between devices, shards(): sums = lax.all_to_all(sums, ('tm', 'height'), 0, 0, tiled=True)  6.43 us
    ppermute x3, starting transfers between devices, shards(): received.append(lax.ppermute(latent, ('tm', 'height'), route))  5.91 us
    ppermute x1, starting transfers between devices, shards(): other = lax.ppermute(own, 'height', [(i, i ^ 1) for i in range(height)])  5 us
    pallas_call x1, Pallas kernels, shards(): pl.pallas_call(functools.partial(opened_kernel, rows), out_shape=(pltpu.V...  3.65 us
    pallas_call x1, Pallas kernels, shards(): pl.pallas_call(functools.partial(stats_kernel, rows), out_shape=jax.Shape...  2.29 us
    ppermute x3, waiting for transfers between devices, shards(): received.append(lax.ppermute(latent, ('tm', 'height'), route))  2.2 us
    slice x1, local copies, waits for them, and re-layouts, shards(): conv_weight[:6 * channels]  1.66 us
  transfers between devices with their start and end apart: 6, of which 3 were waited for; matrix products, arithmetic and copies ran while one was open for 4% of the time, Pallas kernels for 11%

profile of v2, /device:TPU:0, one launch (start us, length us, event | category | flops | bytes accessed | tf_op | source)
XLA Modules:
  0.0 44.8 jit_solution(2301440382964684340)
XLA Ops:
  0.0 3.0 %collective-permute-start = (bf16[6,2560]{1,0:T(8,128)(2,1)}, bf16[6,2560]{1,0:T(8,128)(2,1)S(1)}, u32[]{:S(2)}, u32[]{:S(2)}) collective-permute-start(bf16[6,2560]{1,0:T(8,128)(2,1)} %param.7), channel_id=1, source_target_pairs={{0,16},{1,18},{2,20},{3,22},{4,17},{5,19},{6,21},{7,23},{8,24},{9,... | collective-permute-start | bytes 92168 | tf_op jit(solution)/shard_map/ppermute | solution.py:370
  3.0 1.5 %collective-permute-start.1 = (bf16[6,2560]{1,0:T(8,128)(2,1)}, bf16[6,2560]{1,0:T(8,128)(2,1)S(1)}, u32[]{:S(2)}, u32[]{:S(2)}) collective-permute-start(bf16[6,2560]{1,0:T(8,128)(2,1)} %param.7), channel_id=1, source_target_pairs={{0,8},{1,10},{2,12},{3,14},{4,9},{5,11},{6,13},{7,15},{8,16},{9,18... | collective-permute-start | bytes 92168 | tf_op jit(solution)/shard_map/ppermute | solution.py:370
  4.5 1.4 %collective-permute-start.2 = (bf16[6,2560]{1,0:T(8,128)(2,1)}, bf16[6,2560]{1,0:T(8,128)(2,1)S(1)}, u32[]{:S(2)}, u32[]{:S(2)}) collective-permute-start(bf16[6,2560]{1,0:T(8,128)(2,1)} %param.7), channel_id=1, source_target_pairs={{0,0},{1,2},{2,4},{3,6},{4,1},{5,3},{6,5},{7,7},{8,8},{9,10},{10,1... | collective-permute-start | bytes 92168 | tf_op jit(solution)/shard_map/ppermute | solution.py:370
  5.9 0.0 collective-permute-done
  5.9 2.2 %collective-permute-done.1 = bf16[6,2560]{1,0:T(8,128)(2,1)S(1)} collective-permute-done((bf16[6,2560]{1,0:T(8,128)(2,1)}, bf16[6,2560]{1,0:T(8,128)(2,1)S(1)}, u32[]{:S(2)}, u32[]{:S(2)}) %collective-permute-start.1) | collective-permute-done | bytes 30752 | tf_op jit(solution)/shard_map/ppermute | solution.py:370
  8.1 0.0 collective-permute-done.2
  8.1 5.0 %collective-permute-start.3 = (bf16[3,6,2560]{2,1,0:T(8,128)(2,1)S(1)}, bf16[3,6,2560]{2,1,0:T(8,128)(2,1)S(1)}, u32[]{:S(2)}, u32[]{:S(2)}) collective-permute-start(bf16[3,6,2560]{2,1,0:T(8,128)(2,1)S(1)} %get-tuple-element.14.own_ref), channel_id=1, source_target_pairs={{0,1},{1,0},{2,3},{3,2},{4,5},{5,4},{6,7},{7,6},{8,9},{9,8},{10,11... | collective-permute-start | bytes 276488 | tf_op jit(solution)/shard_map/ppermute | solution.py:372
  13.1 1.0 %collective-permute-done.3.other_ref = bf16[3,6,2560]{2,1,0:T(8,128)(2,1)S(1)} collective-permute-done((bf16[3,6,2560]{2,1,0:T(8,128)(2,1)S(1)}, bf16[3,6,2560]{2,1,0:T(8,128)(2,1)S(1)}, u32[]{:S(2)}, u32[]{:S(2)}) %collective-permute-start.3) | collective-permute-done | bytes 92192 | tf_op jit(solution)/shard_map/ppermute | solution.py:372
  14.1 0.1 fusion
  14.2 0.7 %collective-permute-start.4 = (bf16[2,3,2,2560]{3,2,1,0:T(2,128)(2,1)S(1)}, bf16[2,3,2,2560]{3,2,1,0:T(2,128)(2,1)S(1)}, u32[]{:S(2)}, u32[]{:S(2)}) collective-permute-start(bf16[2,3,2,2560]{3,2,1,0:T(2,128)(2,1)S(1)} %fusion), channel_id=1, source_target_pairs={{1,2},{3,4},{5,6},{2,1},{4,3},{6,5},{9,10},{11,12},{13,14},{10,9},... | collective-permute-start | bytes 184328 | tf_op jit(solution)/shard_map/ppermute | solution.py:375
  14.9 1.1 %band.1 = (bf16[640,768]{1,0:T(8,128)(2,1)S(1)}, f32[4,384]{1,0:T(4,128)S(1)}) custom-call(bf16[432,384]{1,0:T(8,128)(2,1)} %w_ref.1, f32[384]{0:T(512)} %refs_0_.1, f32[384]{0:T(512)} %refs_1_.1, f32[384]{0:T(512)} %refs_2_.1, f32[384]{0:T(512)} %refs_3_.1), custom_call_target="tpu_custom_call" | custom-call | tf_op jit(solution)/shard_map/band/pallas_call | solution.py:353
  16.0 0.0 copy-start
  16.0 0.0 collective-permute-done.4.halo_ref
  16.0 2.3 %stats.1 = f32[32,1,768]{2,1,0:T(1,128)} custom-call(bf16[3,6,2560]{2,1,0:T(8,128)(2,1)S(1)} %get-tuple-element.14.own_ref, bf16[3,6,2560]{2,1,0:T(8,128)(2,1)S(1)} %collective-permute-done.3.other_ref, bf16[2,3,2,2560]{3,2,1,0:T(2,128)(2,1)S(1)} %collective-permute-done.4.halo_ref, bf16[640,768]{1,0:T(8,128)(2,1)S(1)} %get-tuple-element.9.band_ref, ...), custom_call_target="tpu_custom_call" | custom-call | tf_op jit(solution)/shard_map/stats/pallas_call | solution.py:389
  18.3 0.0 copy-done
  18.3 6.4 %all-to-all-start = ((f32[32,1,768]{2,1,0:T(1,128)}), f32[32,1,768]{2,1,0:T(1,128)S(1)}, u32[]{:S(2)}, u32[]{:S(2)}) async-start(f32[32,1,768]{2,1,0:T(1,128)} %stats.1), calls=%async_computation | async-start | bytes 196608 | tf_op jit(solution)/shard_map/all_to_all | solution.py:397
  24.8 1.7 %slice.3.head_ref = bf16[2304,384]{1,0:T(8,128)(2,1)S(1)} slice(bf16[10368,384]{1,0:T(8,128)(2,1)} %w_hbm.1), slice={[0:2304], [0:384]} | slice | bytes 3538944 | tf_op jit(solution)/shard_map/slice | solution.py:413
  26.4 0.0 copy-start.1
  26.4 1.2 %copy-done.1 = bf16[640,768]{1,0:T(8,128)(2,1)S(1)} copy-done((bf16[640,768]{1,0:T(8,128)(2,1)S(1)}, bf16[640,768]{1,0:T(8,128)(2,1)}, u32[]{:S(2)}) %copy-start.1) | copy-done | bytes 983064
  27.6 3.7 %opened.1 = (f32[5,10,16,384]{3,2,1,0:T(8,128)S(1)}, f32[3,5,10,16,384]{4,3,2,1,0:T(8,128)}) custom-call(bf16[3,6,2560]{2,1,0:T(8,128)(2,1)S(1)} %get-tuple-element.14.own_ref, bf16[3,6,2560]{2,1,0:T(8,128)(2,1)S(1)} %collective-permute-done.3.other_ref, bf16[2,3,2,2560]{3,2,1,0:T(2,128)(2,1)S(1)} %collective-permute-done.4.halo_ref, ...), custom_call_target="tpu_custom_call" | custom-call | flops 1572864000 | bytes 4915200 | tf_op jit(solution)/shard_map/opened/pallas_call | solution.py:400
  31.3 1.0 %all-to-all-done.sum_ref = f32[32,1,768]{2,1,0:T(1,128)S(1)} async-done(((f32[32,1,768]{2,1,0:T(1,128)}), f32[32,1,768]{2,1,0:T(1,128)S(1)}, u32[]{:S(2)}, u32[]{:S(2)}) %all-to-all-start) | async-done | bytes 98336 | tf_op jit(solution)/shard_map/all_to_all | solution.py:397
  32.3 12.3 %second.1 = bf16[2,3,160,384]{3,2,1,0:T(8,128)(2,1)} custom-call(f32[32,1,768]{2,1,0:T(1,128)S(1)} %all-to-all-done.sum_ref, f32[5,10,16,384]{3,2,1,0:T(8,128)S(1)} %get-tuple-element.11.first_ref, f32[3,5,10,16,384]{4,3,2,1,0:T(8,128)} %get-tuple-element.12.o_hbm, bf16[2304,384]{1,0:T(8,128)(2,1)S(1)} %slice.3.head_ref, bf16[10368,384]{1,0:T(8,128)(2,1)} %w_hbm.1, ...), custom_call_target="tpu_custom_call" | custom-call | tf_op jit(solution)/shard_map/second/pallas_call | solution.py:326
  (1 shorter events, 0.0 us)
Async XLA Ops:
  0.0 5.9 %collective-permute-start = (bf16[6,2560]{1,0:T(8,128)(2,1)}, bf16[6,2560]{1,0:T(8,128)(2,1)S(1)}, u32[]{:S(2)}, u32[]{:S(2)}) collective-permute-start(bf16[6,2560]{1,0:T(8,128)(2,1)} %param.7), channel_id=1, source_target_pairs={{0,16},{1,18},{2,20},{3,22},{4,17},{5,19},{6,21},{7,23},{8,24},{9,... | collective-permute-start | bytes 92168 | tf_op jit(solution)/shard_map/ppermute | solution.py:370
  3.0 5.1 %collective-permute-start.1 = (bf16[6,2560]{1,0:T(8,128)(2,1)}, bf16[6,2560]{1,0:T(8,128)(2,1)S(1)}, u32[]{:S(2)}, u32[]{:S(2)}) collective-permute-start(bf16[6,2560]{1,0:T(8,128)(2,1)} %param.7), channel_id=1, source_target_pairs={{0,8},{1,10},{2,12},{3,14},{4,9},{5,11},{6,13},{7,15},{8,16},{9,18... | collective-permute-start | bytes 92168 | tf_op jit(solution)/shard_map/ppermute | solution.py:370
  4.5 3.6 %collective-permute-start.2 = (bf16[6,2560]{1,0:T(8,128)(2,1)}, bf16[6,2560]{1,0:T(8,128)(2,1)S(1)}, u32[]{:S(2)}, u32[]{:S(2)}) collective-permute-start(bf16[6,2560]{1,0:T(8,128)(2,1)} %param.7), channel_id=1, source_target_pairs={{0,0},{1,2},{2,4},{3,6},{4,1},{5,3},{6,5},{7,7},{8,8},{9,10},{10,1... | collective-permute-start | bytes 92168 | tf_op jit(solution)/shard_map/ppermute | solution.py:370
  8.1 6.0 %collective-permute-start.3 = (bf16[3,6,2560]{2,1,0:T(8,128)(2,1)S(1)}, bf16[3,6,2560]{2,1,0:T(8,128)(2,1)S(1)}, u32[]{:S(2)}, u32[]{:S(2)}) collective-permute-start(bf16[3,6,2560]{2,1,0:T(8,128)(2,1)S(1)} %get-tuple-element.14.own_ref), channel_id=1, source_target_pairs={{0,1},{1,0},{2,3},{3,2},{4,5},{5,4},{6,7},{7,6},{8,9},{9,8},{10,11... | collective-permute-start | bytes 276488 | tf_op jit(solution)/shard_map/ppermute | solution.py:372
  14.2 1.8 %collective-permute-start.4 = (bf16[2,3,2,2560]{3,2,1,0:T(2,128)(2,1)S(1)}, bf16[2,3,2,2560]{3,2,1,0:T(2,128)(2,1)S(1)}, u32[]{:S(2)}, u32[]{:S(2)}) collective-permute-start(bf16[2,3,2,2560]{3,2,1,0:T(2,128)(2,1)S(1)} %fusion), channel_id=1, source_target_pairs={{1,2},{3,4},{5,6},{2,1},{4,3},{6,5},{9,10},{11,12},{13,14},{10,9},... | collective-permute-start | bytes 184328 | tf_op jit(solution)/shard_map/ppermute | solution.py:375
  16.0 2.3 %copy-start = (bf16[640,768]{1,0:T(8,128)(2,1)}, bf16[640,768]{1,0:T(8,128)(2,1)S(1)}, u32[]{:S(2)}) copy-start(bf16[640,768]{1,0:T(8,128)(2,1)S(1)} %get-tuple-element.9.band_ref) | copy-start | bytes 2949124
  18.3 14.0 %all-to-all-start = ((f32[32,1,768]{2,1,0:T(1,128)}), f32[32,1,768]{2,1,0:T(1,128)S(1)}, u32[]{:S(2)}, u32[]{:S(2)}) async-start(f32[32,1,768]{2,1,0:T(1,128)} %stats.1), calls=%async_computation | async-start | bytes 196608 | tf_op jit(solution)/shard_map/all_to_all | solution.py:397
  26.4 1.2 %copy-start.1 = (bf16[640,768]{1,0:T(8,128)(2,1)S(1)}, bf16[640,768]{1,0:T(8,128)(2,1)}, u32[]{:S(2)}) copy-start(bf16[640,768]{1,0:T(8,128)(2,1)} %copy-done) | copy-start | bytes 2949124

commit v3 on v2

--- a/solution.py
+++ b/solution.py
@@ -49,13 +49,14 @@
     return copies
 
 
-def lay_out(rows, own_ref, other_ref, halo_ref, z_ref, e_ref, f_ref):
+def lay_out(rows, distances, own_ref, other_ref, halo_ref, z_ref, e_ref, f_ref):
     core = lax.rem(lax.axis_index("height"), 2)
     slots = 3 * rows
     per = COLS // SEG
     high = rows + 2
 
-    for frame in range(6):
+    frames = range(2 * distances[0], 6)
+    for frame in frames:
         for slot in (0, slots - 1):
             row = (frame * slots + slot) * SEG
             for half in range(2):
@@ -77,17 +78,18 @@
 
     main = jnp.where(core == 0, rows, 0)
     edge_slot = jnp.where(core == 0, rows - 2, 2 * rows)
-    for d in range(3):
+    row_block, last_block = lax.axis_index("height"), lax.axis_size("height") - 1
+    beside = jnp.where(core == 0, row_block > 0, row_block < last_block)
+    for d in distances:
         real = lax.axis_index("tm") >= 2 - d
 
-        def piece(ref, *index):
-            x = ref[(*index, d)].astype(F32)
-            return x if d == 2 else jnp.where(real, x, 0.0)
-
-        spread(piece(own_ref), 2 * d + core, main)
-        spread(piece(other_ref), 2 * d + 1 - core, main)
-        spread(piece(halo_ref, 0), 2 * d + 1 - core, edge_slot)
-        spread(piece(halo_ref, 1), 2 * d + core, edge_slot)
+        def piece(ref, keep, *index):
+            return jnp.where(keep, ref[(*index, d)].astype(F32), 0.0)
+
+        spread(piece(own_ref, real), 2 * d + core, main)
+        spread(piece(other_ref, real), 2 * d + 1 - core, main)
+        spread(piece(halo_ref, real & beside, 0), 2 * d + core, edge_slot)
+        spread(piece(halo_ref, real & beside, 1), 2 * d + 1 - core, edge_slot)
 
     first = rows - 2
     span = rows + 4
@@ -99,11 +101,11 @@
 
     for pair, (half, offset) in enumerate(where):
         upper = []
-        for frame in range(6):
+        for frame in frames:
             x = z_ref[half, pl.ds((frame * slots + first) * SEG, (span + 1) * SEG), :]
             low, up = turned(x, -offset), turned(x, LANES // 2 - offset)
             e_ref[pair, frame] = jnp.where(low_side, low[: span * SEG], up[SEG:]).astype(BF16)
-            if 0 < frame < 5:
+            if frames[0] < frame < 5:
                 f_ref[pair, frame - 1] = jnp.where(
                     low_side[: high * SEG], upper, up[2 * SEG : span * SEG]
                 ).astype(BF16)
@@ -111,7 +113,7 @@
 
 
 def stats_kernel(rows, own_ref, other_ref, halo_ref, band_ref, v_ref, sum_ref, z_ref, e_ref, f_ref):
-    lay_out(rows, own_ref, other_ref, halo_ref, z_ref, e_ref, f_ref)
+    lay_out(rows, (1, 2), own_ref, other_ref, halo_ref, z_ref, e_ref, f_ref)
     channels = v_ref.shape[1]
     per = COLS // SEG
     sums = jnp.zeros((8, 2 * channels), F32)
@@ -133,7 +135,7 @@
 def opened_kernel(
     rows, own_ref, other_ref, halo_ref, band_ref, v_ref, first_ref, o_hbm, z_ref, e_ref, f_ref, o_ref, sem
 ):
-    lay_out(rows, own_ref, other_ref, halo_ref, z_ref, e_ref, f_ref)
+    lay_out(rows, (0, 1, 2), own_ref, other_ref, halo_ref, z_ref, e_ref, f_ref)
     channels = v_ref.shape[1]
     high = rows + 2
     stores = []
@@ -309,7 +311,9 @@
     wait1 = functools.partial(need, weights[0], loads[0])
     wait2 = functools.partial(need, *weights[1:4], loads[1])
     wait3 = functools.partial(need, *weights[4:], loads[2])
-    edge(0, 0, [((0, 1), steps([], [wait1])), ((2,), steps(rows1, [wait2]))])
+    wait3a = functools.partial(need, *weights[4:])
+    wait3b = functools.partial(need, loads[2])
+    edge(0, 0, [((0, 1), steps([], [], [wait1])), ((2,), steps(rows1, [wait2]))])
     shared(1, steps(rows2, [wait3]))
     shared(2, steps(rows3))
     first = finish(0)
@@ -370,9 +374,10 @@
         received.append(lax.ppermute(latent, ("tm", "height"), route))
     own = jnp.stack(received)
     other = lax.ppermute(own, "height", [(i, i ^ 1) for i in range(height)])
-    edge = lax.dynamic_slice_in_dim(jnp.stack([own, other]), core * (2 * rows - 2), 2, axis=2)
-    swap = [(2 * m - 1, 2 * m) for m in range(1, half)] + [(2 * m, 2 * m - 1) for m in range(1, half)]
-    halo = lax.ppermute(edge, "height", swap)
+    edge = lax.dynamic_slice_in_dim(jnp.stack([own, other]), (1 - core) * (2 * rows - 2), 2, axis=2)
+    down = [(2 * m, 2 * m + 2) for m in range(half - 1)] + [(height - 2, height - 1)]
+    up = [(2 * m + 1, 2 * m - 1) for m in range(1, half)] + [(1, 0)]
+    halo = lax.ppermute(edge, "height", down + up)
 
     per = COLS // SEG
     high = rows + 2

time: 45.1 us -> 43.3 us (0.960)
  starting transfers between devices: 18 us -> 15.8 us
  waiting for transfers between devices: 4.22 us -> 5.18 us
    all_to_all x1, starting transfers between devices: 6.43 us -> 4.88 us  [shards(): sums = lax.all_to_all(sums, ('tm', 'height'), 0, 0, tiled=True)]
    ppermute x1, waiting for transfers between devices: 0.01 us -> 0.72 us  [shards(): halo = lax.ppermute(edge, 'height', down + up)]
    ppermute x1, starting transfers between devices: 0.66 us -> 0.02 us  [shards(): halo = lax.ppermute(edge, 'height', down + up)]
  transfers between devices with their start and end apart: 6 -> 6, of which waited for: 3 -> 4; matrix products, arithmetic and copies ran while one was open for 4% -> 4% of each run, Pallas kernels for 11% -> 11%
where the time goes in v3:
time: 43.3 us; the launch traced here: 43 us
  Pallas kernels  19 us (44%)
  starting transfers between devices  15.8 us (36%)
  waiting for transfers between devices  5.18 us (12%)
  local copies, waits for them, and re-layouts  2.86 us (7%)
    pallas_call x1, Pallas kernels, second_part(): pl.pallas_call(functools.partial(second_kernel, rows, entries), out_shape...  12.4 us
    ppermute x3, starting transfers between devices, shards(): received.append(lax.ppermute(latent, ('tm', 'height'), route))  5.91 us
    ppermute x1, starting transfers between devices, shards(): other = lax.ppermute(own, 'height', [(i, i ^ 1) for i in range(height)])  5 us
    all_to_all x1, starting transfers between devices, shards(): sums = lax.all_to_all(sums, ('tm', 'height'), 0, 0, tiled=True)  4.88 us
    pallas_call x1, Pallas kernels, shards(): pl.pallas_call(functools.partial(opened_kernel, rows), out_shape=(pltpu.V...  3.61 us
    ppermute x3, waiting for transfers between devices, shards(): received.append(lax.ppermute(latent, ('tm', 'height'), route))  2.2 us
    pallas_call x1, Pallas kernels, shards(): pl.pallas_call(functools.partial(stats_kernel, rows), out_shape=jax.Shape...  1.89 us
    slice x1, local copies, waits for them, and re-layouts, shards(): conv_weight[:6 * channels]  1.66 us
  transfers between devices with their start and end apart: 6, of which 4 were waited for; matrix products, arithmetic and copies ran while one was open for 4% of the time, Pallas kernels for 11%

profile of v3, /device:TPU:0, one launch (start us, length us, event | category | flops | bytes accessed | tf_op | source)
XLA Modules:
  0.0 43.0 jit_solution(15536419194810773327)
XLA Ops:
  0.0 3.0 %collective-permute-start = (bf16[6,2560]{1,0:T(8,128)(2,1)}, bf16[6,2560]{1,0:T(8,128)(2,1)S(1)}, u32[]{:S(2)}, u32[]{:S(2)}) collective-permute-start(bf16[6,2560]{1,0:T(8,128)(2,1)} %param.7), channel_id=1, source_target_pairs={{0,16},{1,18},{2,20},{3,22},{4,17},{5,19},{6,21},{7,23},{8,24},{9,... | collective-permute-start | bytes 92168 | tf_op jit(solution)/shard_map/ppermute | solution.py:374
  3.0 1.5 %collective-permute-start.1 = (bf16[6,2560]{1,0:T(8,128)(2,1)}, bf16[6,2560]{1,0:T(8,128)(2,1)S(1)}, u32[]{:S(2)}, u32[]{:S(2)}) collective-permute-start(bf16[6,2560]{1,0:T(8,128)(2,1)} %param.7), channel_id=1, source_target_pairs={{0,8},{1,10},{2,12},{3,14},{4,9},{5,11},{6,13},{7,15},{8,16},{9,18... | collective-permute-start | bytes 92168 | tf_op jit(solution)/shard_map/ppermute | solution.py:374
  4.5 1.4 %collective-permute-start.2 = (bf16[6,2560]{1,0:T(8,128)(2,1)}, bf16[6,2560]{1,0:T(8,128)(2,1)S(1)}, u32[]{:S(2)}, u32[]{:S(2)}) collective-permute-start(bf16[6,2560]{1,0:T(8,128)(2,1)} %param.7), channel_id=1, source_target_pairs={{0,0},{1,2},{2,4},{3,6},{4,1},{5,3},{6,5},{7,7},{8,8},{9,10},{10,1... | collective-permute-start | bytes 92168 | tf_op jit(solution)/shard_map/ppermute | solution.py:374
  5.9 0.0 collective-permute-done
  5.9 2.2 %collective-permute-done.1 = bf16[6,2560]{1,0:T(8,128)(2,1)S(1)} collective-permute-done((bf16[6,2560]{1,0:T(8,128)(2,1)}, bf16[6,2560]{1,0:T(8,128)(2,1)S(1)}, u32[]{:S(2)}, u32[]{:S(2)}) %collective-permute-start.1) | collective-permute-done | bytes 30752 | tf_op jit(solution)/shard_map/ppermute | solution.py:374
  8.1 0.0 collective-permute-done.2
  8.1 5.0 %collective-permute-start.3 = (bf16[3,6,2560]{2,1,0:T(8,128)(2,1)S(1)}, bf16[3,6,2560]{2,1,0:T(8,128)(2,1)S(1)}, u32[]{:S(2)}, u32[]{:S(2)}) collective-permute-start(bf16[3,6,2560]{2,1,0:T(8,128)(2,1)S(1)} %get-tuple-element.14.own_ref), channel_id=1, source_target_pairs={{0,1},{1,0},{2,3},{3,2},{4,5},{5,4},{6,7},{7,6},{8,9},{9,8},{10,11... | collective-permute-start | bytes 276488 | tf_op jit(solution)/shard_map/ppermute | solution.py:376
  13.1 1.0 %collective-permute-done.3.other_ref = bf16[3,6,2560]{2,1,0:T(8,128)(2,1)S(1)} collective-permute-done((bf16[3,6,2560]{2,1,0:T(8,128)(2,1)S(1)}, bf16[3,6,2560]{2,1,0:T(8,128)(2,1)S(1)}, u32[]{:S(2)}, u32[]{:S(2)}) %collective-permute-start.3) | collective-permute-done | bytes 92192 | tf_op jit(solution)/shard_map/ppermute | solution.py:376
  14.1 0.1 fusion
  14.2 0.0 collective-permute-start.4
  14.2 1.1 %band.1 = (bf16[640,768]{1,0:T(8,128)(2,1)S(1)}, f32[4,384]{1,0:T(4,128)S(1)}) custom-call(bf16[432,384]{1,0:T(8,128)(2,1)} %w_ref.1, f32[384]{0:T(512)} %refs_0_.1, f32[384]{0:T(512)} %refs_1_.1, f32[384]{0:T(512)} %refs_2_.1, f32[384]{0:T(512)} %refs_3_.1), custom_call_target="tpu_custom_call" | custom-call | tf_op jit(solution)/shard_map/band/pallas_call | solution.py:357
  15.4 0.0 copy-start
  15.4 0.7 %collective-permute-done.4.halo_ref = bf16[2,3,2,2560]{3,2,1,0:T(2,128)(2,1)S(1)} collective-permute-done((bf16[2,3,2,2560]{3,2,1,0:T(2,128)(2,1)S(1)}, bf16[2,3,2,2560]{3,2,1,0:T(2,128)(2,1)S(1)}, u32[]{:S(2)}, u32[]{:S(2)}) %collective-permute-start.4) | collective-permute-done | bytes 61472 | tf_op jit(solution)/shard_map/ppermute | solution.py:380
  16.1 1.9 %stats.1 = f32[32,1,768]{2,1,0:T(1,128)} custom-call(bf16[3,6,2560]{2,1,0:T(8,128)(2,1)S(1)} %get-tuple-element.14.own_ref, bf16[3,6,2560]{2,1,0:T(8,128)(2,1)S(1)} %collective-permute-done.3.other_ref, bf16[2,3,2,2560]{3,2,1,0:T(2,128)(2,1)S(1)} %collective-permute-done.4.halo_ref, bf16[640,768]{1,0:T(8,128)(2,1)S(1)} %get-tuple-element.9.band_ref, ...), custom_call_target="tpu_custom_call" | custom-call | tf_op jit(solution)/shard_map/stats/pallas_call | solution.py:394
  18.0 0.0 copy-done
  18.0 4.9 %all-to-all-start = ((f32[32,1,768]{2,1,0:T(1,128)}), f32[32,1,768]{2,1,0:T(1,128)S(1)}, u32[]{:S(2)}, u32[]{:S(2)}) async-start(f32[32,1,768]{2,1,0:T(1,128)} %stats.1), calls=%async_computation | async-start | bytes 196608 | tf_op jit(solution)/shard_map/all_to_all | solution.py:402
  22.9 1.7 %slice.3.head_ref = bf16[2304,384]{1,0:T(8,128)(2,1)S(1)} slice(bf16[10368,384]{1,0:T(8,128)(2,1)} %w_hbm.1), slice={[0:2304], [0:384]} | slice | bytes 3538944 | tf_op jit(solution)/shard_map/slice | solution.py:418
  24.5 0.0 copy-start.1
  24.6 1.2 %copy-done.1 = bf16[640,768]{1,0:T(8,128)(2,1)S(1)} copy-done((bf16[640,768]{1,0:T(8,128)(2,1)S(1)}, bf16[640,768]{1,0:T(8,128)(2,1)}, u32[]{:S(2)}) %copy-start.1) | copy-done | bytes 983064
  25.7 3.6 %opened.1 = (f32[5,10,16,384]{3,2,1,0:T(8,128)S(1)}, f32[3,5,10,16,384]{4,3,2,1,0:T(8,128)}) custom-call(bf16[3,6,2560]{2,1,0:T(8,128)(2,1)S(1)} %get-tuple-element.14.own_ref, bf16[3,6,2560]{2,1,0:T(8,128)(2,1)S(1)} %collective-permute-done.3.other_ref, bf16[2,3,2,2560]{3,2,1,0:T(2,128)(2,1)S(1)} %collective-permute-done.4.halo_ref, ...), custom_call_target="tpu_custom_call" | custom-call | flops 1572864000 | bytes 4915200 | tf_op jit(solution)/shard_map/opened/pallas_call | solution.py:405
  29.4 1.3 %all-to-all-done.sum_ref = f32[32,1,768]{2,1,0:T(1,128)S(1)} async-done(((f32[32,1,768]{2,1,0:T(1,128)}), f32[32,1,768]{2,1,0:T(1,128)S(1)}, u32[]{:S(2)}, u32[]{:S(2)}) %all-to-all-start) | async-done | bytes 98336 | tf_op jit(solution)/shard_map/all_to_all | solution.py:402
  30.6 12.4 %second.1 = bf16[2,3,160,384]{3,2,1,0:T(8,128)(2,1)} custom-call(f32[32,1,768]{2,1,0:T(1,128)S(1)} %all-to-all-done.sum_ref, f32[5,10,16,384]{3,2,1,0:T(8,128)S(1)} %get-tuple-element.11.first_ref, f32[3,5,10,16,384]{4,3,2,1,0:T(8,128)} %get-tuple-element.12.o_hbm, bf16[2304,384]{1,0:T(8,128)(2,1)S(1)} %slice.3.head_ref, bf16[10368,384]{1,0:T(8,128)(2,1)} %w_hbm.1, ...), custom_call_target="tpu_custom_call" | custom-call | tf_op jit(solution)/shard_map/second/pallas_call | solution.py:330
  (1 shorter events, 0.0 us)
Async XLA Ops:
  0.0 5.9 %collective-permute-start = (bf16[6,2560]{1,0:T(8,128)(2,1)}, bf16[6,2560]{1,0:T(8,128)(2,1)S(1)}, u32[]{:S(2)}, u32[]{:S(2)}) collective-permute-start(bf16[6,2560]{1,0:T(8,128)(2,1)} %param.7), channel_id=1, source_target_pairs={{0,16},{1,18},{2,20},{3,22},{4,17},{5,19},{6,21},{7,23},{8,24},{9,... | collective-permute-start | bytes 92168 | tf_op jit(solution)/shard_map/ppermute | solution.py:374
  3.0 5.1 %collective-permute-start.1 = (bf16[6,2560]{1,0:T(8,128)(2,1)}, bf16[6,2560]{1,0:T(8,128)(2,1)S(1)}, u32[]{:S(2)}, u32[]{:S(2)}) collective-permute-start(bf16[6,2560]{1,0:T(8,128)(2,1)} %param.7), channel_id=1, source_target_pairs={{0,8},{1,10},{2,12},{3,14},{4,9},{5,11},{6,13},{7,15},{8,16},{9,18... | collective-permute-start | bytes 92168 | tf_op jit(solution)/shard_map/ppermute | solution.py:374
  4.5 3.6 %collective-permute-start.2 = (bf16[6,2560]{1,0:T(8,128)(2,1)}, bf16[6,2560]{1,0:T(8,128)(2,1)S(1)}, u32[]{:S(2)}, u32[]{:S(2)}) collective-permute-start(bf16[6,2560]{1,0:T(8,128)(2,1)} %param.7), channel_id=1, source_target_pairs={{0,0},{1,2},{2,4},{3,6},{4,1},{5,3},{6,5},{7,7},{8,8},{9,10},{10,1... | collective-permute-start | bytes 92168 | tf_op jit(solution)/shard_map/ppermute | solution.py:374
  8.1 6.0 %collective-permute-start.3 = (bf16[3,6,2560]{2,1,0:T(8,128)(2,1)S(1)}, bf16[3,6,2560]{2,1,0:T(8,128)(2,1)S(1)}, u32[]{:S(2)}, u32[]{:S(2)}) collective-permute-start(bf16[3,6,2560]{2,1,0:T(8,128)(2,1)S(1)} %get-tuple-element.14.own_ref), channel_id=1, source_target_pairs={{0,1},{1,0},{2,3},{3,2},{4,5},{5,4},{6,7},{7,6},{8,9},{9,8},{10,11... | collective-permute-start | bytes 276488 | tf_op jit(solution)/shard_map/ppermute | solution.py:376
  14.2 1.9 %collective-permute-start.4 = (bf16[2,3,2,2560]{3,2,1,0:T(2,128)(2,1)S(1)}, bf16[2,3,2,2560]{3,2,1,0:T(2,128)(2,1)S(1)}, u32[]{:S(2)}, u32[]{:S(2)}) collective-permute-start(bf16[2,3,2,2560]{3,2,1,0:T(2,128)(2,1)S(1)} %fusion), channel_id=1, source_target_pairs={{0,2},{2,4},{4,6},{6,7},{3,1},{5,3},{7,5},{1,0},{8,10},{10,12},{12... | collective-permute-start | bytes 184328 | tf_op jit(solution)/shard_map/ppermute | solution.py:380
  15.4 2.6 %copy-start = (bf16[640,768]{1,0:T(8,128)(2,1)}, bf16[640,768]{1,0:T(8,128)(2,1)S(1)}, u32[]{:S(2)}) copy-start(bf16[640,768]{1,0:T(8,128)(2,1)S(1)} %get-tuple-element.9.band_ref) | copy-start | bytes 2949124
  18.0 12.6 %all-to-all-start = ((f32[32,1,768]{2,1,0:T(1,128)}), f32[32,1,768]{2,1,0:T(1,128)S(1)}, u32[]{:S(2)}, u32[]{:S(2)}) async-start(f32[32,1,768]{2,1,0:T(1,128)} %stats.1), calls=%async_computation | async-start | bytes 196608 | tf_op jit(solution)/shard_map/all_to_all | solution.py:402
  24.5 1.2 %copy-start.1 = (bf16[640,768]{1,0:T(8,128)(2,1)S(1)}, bf16[640,768]{1,0:T(8,128)(2,1)}, u32[]{:S(2)}) copy-start(bf16[640,768]{1,0:T(8,128)(2,1)} %copy-done) | copy-start | bytes 2949124

commit v4 on v3

--- a/solution.py
+++ b/solution.py
@@ -110,6 +110,18 @@
                     low_side[: high * SEG], upper, up[2 * SEG : span * SEG]
                 ).astype(BF16)
             upper = low[2 * SEG : span * SEG]
+
+
+def exact_product(rows, member):
+    parts = []
+    for x in rows:
+        for _ in range(3):
+            part = x.astype(BF16).astype(F32)
+            parts.append(part)
+            x = x - part
+    parts.append(jnp.zeros((16 - len(parts), x.shape[1]), F32))
+    out = jnp.dot(jnp.concatenate(parts, axis=0).astype(BF16), member.astype(BF16), preferred_element_type=F32)
+    return [out[3 * i : 3 * i + 1] + out[3 * i + 1 : 3 * i + 2] + out[3 * i + 2 : 3 * i + 3] for i in range(len(rows))]
 
 
 def stats_kernel(rows, own_ref, other_ref, halo_ref, band_ref, v_ref, sum_ref, z_ref, e_ref, f_ref):
@@ -126,10 +138,18 @@
         out = (out + bias).reshape(-1, 8, 2 * channels)
         sums = sums + jnp.sum(out, axis=0)
         squares = squares + jnp.sum(out * out, axis=0)
-    for i, part in enumerate((sums, squares)):
-        whole = jnp.sum(part, axis=0, keepdims=True)
-        whole = whole[:, :channels] + whole[:, channels:]
-        sum_ref[:, 0, i * channels : (i + 1) * channels] = jnp.broadcast_to(whole, (sum_ref.shape[0], channels))
+    whole = []
+    for part in (sums, squares):
+        row = jnp.sum(part, axis=0, keepdims=True)
+        whole.append(row[:, :channels] + row[:, channels:])
+    size = channels // GROUPS
+    row = lax.broadcasted_iota(jnp.int32, (channels, LANES), 0)
+    first = lax.rem(lax.broadcasted_iota(jnp.int32, (channels, LANES), 1), GROUPS) * size
+    member = jnp.where((row >= first) & (row < first + size), 1.0, 0.0)
+    per_group = exact_product(whole, member)
+    lane = lax.broadcasted_iota(jnp.int32, (1, LANES), 1)
+    payload = jnp.where(lane < GROUPS, per_group[0], per_group[1])
+    sum_ref[:, 0, :] = jnp.broadcast_to(payload, (sum_ref.shape[0], LANES))
 
 
 def opened_kernel(
@@ -174,16 +194,17 @@
         copy.start()
     height = lax.axis_index("height")
     frame = lax.axis_index("tm")
-    group = channels // GROUPS
-    left = jnp.floor((lax.broadcasted_iota(jnp.int32, (channels, channels), 0).astype(F32) + 0.5) / group)
-    right = jnp.floor((lax.broadcasted_iota(jnp.int32, (channels, channels), 1).astype(F32) + 0.5) / group)
-    same = jnp.where(left == right, 1.0, 0.0).astype(F32)
+    size = channels // GROUPS
+    lane = lax.broadcasted_iota(jnp.int32, (1, LANES), 1)
     total = jnp.sum(sum_ref[:, 0, :], axis=0, keepdims=True)
-    both = jnp.concatenate([total[:, :channels], total[:, channels:], jnp.zeros((6, channels), F32)], axis=0)
-    totals = jnp.dot(both, same, precision=lax.Precision.HIGHEST, preferred_element_type=F32)
-    mean = totals[0:1] / entries
-    var = totals[1:2] / entries - mean * mean
-    scale = lax.rsqrt(var + 1e-06) * v_ref[1:2, :]
+    mean = total / entries
+    var = pltpu.roll(mean, LANES - GROUPS, 1) - mean * mean
+    inverse = lax.rsqrt(jnp.where(lane < GROUPS, var, 1.0) + 1e-06)
+    first = lax.broadcasted_iota(jnp.int32, (LANES, channels), 0) * size
+    column = lax.broadcasted_iota(jnp.int32, (LANES, channels), 1)
+    member = jnp.where((column >= first) & (column < first + size), 1.0, 0.0)
+    mean, inverse = exact_product([mean, inverse], member)
+    scale = inverse * v_ref[1:2, :]
     half_scale = 0.5 * scale
     half_shift = 0.5 * (v_ref[2:3, :] - mean * scale)
     lane_row = lax.broadcasted_iota(jnp.int32, (SEG, channels), 0)
@@ -393,12 +414,13 @@
     ]
     sums = pl.pallas_call(
         functools.partial(stats_kernel, rows),
-        out_shape=jax.ShapeDtypeStruct((tm * height, 1, 2 * channels), F32),
+        out_shape=jax.ShapeDtypeStruct((tm * height, 1, LANES), F32),
         in_specs=[vmem] * 5,
         scratch_shapes=scratch,
         compiler_params=pltpu.CompilerParams(vmem_limit_bytes=12 << 20),
         name="stats",
     )(own, other, halo, band, vectors)
+    sums, later_weight = lax.optimization_barrier((sums, conv_weight))
     sums = lax.all_to_all(sums, ("tm", "height"), 0, 0, tiled=True)
     positions = 4 * high * per * SEG
     opened_shape = (3, high, per, SEG, channels)
@@ -415,7 +437,7 @@
         name="opened",
     )(own, other, halo, band, vectors)
     entries = frames * tm * rows * height * COLS * (channels // GROUPS)
-    head = pltpu.with_memory_space_constraint(conv_weight[: 6 * channels], pltpu.VMEM)
+    head = pltpu.with_memory_space_constraint(later_weight[: 6 * channels], pltpu.VMEM)
     return second_part(rows, entries, sums, first, keep(opened), head, keep(conv_weight), vectors)
 
 

time: 43.3 us -> 42.3 us (0.977)
  local copies, waits for them, and re-layouts: 2.86 us -> 1.66 us
  waiting for transfers between devices: 5.18 us -> 5.7 us
    unnamed x4 -> x0, local copies, waits for them, and re-layouts: 1.2 us -> none
    all_to_all x1, waiting for transfers between devices: 1.28 us -> 1.8 us  [shards(): sums = lax.all_to_all(sums, ('tm', 'height'), 0, 0, tiled=True)]
    pallas_call x1, Pallas kernels: 12.4 us -> 11.9 us  [second_part(): pl.pallas_call(functools.partial(second_kernel, rows, entries), out_shape...]
where the time goes in v4:
time: 42.3 us; the launch traced here: 42.1 us
  Pallas kernels  18.8 us (44%)
  starting transfers between devices  15.8 us (37%)
  waiting for transfers between devices  5.7 us (13%)
  local copies, waits for them, and re-layouts  1.66 us (4%)
    pallas_call x1, Pallas kernels, second_part(): pl.pallas_call(functools.partial(second_kernel, rows, entries), out_shape...  11.9 us
    ppermute x3, starting transfers between devices, shards(): received.append(lax.ppermute(latent, ('tm', 'height'), route))  5.91 us
    ppermute x1, starting transfers between devices, shards(): other = lax.ppermute(own, 'height', [(i, i ^ 1) for i in range(height)])  5 us
    all_to_all x1, starting transfers between devices, shards(): sums = lax.all_to_all(sums, ('tm', 'height'), 0, 0, tiled=True)  4.88 us
    pallas_call x1, Pallas kernels, shards(): pl.pallas_call(functools.partial(opened_kernel, rows), out_shape=(pltpu.V...  3.63 us
    ppermute x3, waiting for transfers between devices, shards(): received.append(lax.ppermute(latent, ('tm', 'height'), route))  2.2 us
    pallas_call x1, Pallas kernels, shards(): pl.pallas_call(functools.partial(stats_kernel, rows), out_shape=jax.Shape...  2.09 us
    all_to_all x1, waiting for transfers between devices, shards(): sums = lax.all_to_all(sums, ('tm', 'height'), 0, 0, tiled=True)  1.8 us
  transfers between devices with their start and end apart: 6, of which 4 were waited for; matrix products, arithmetic and copies ran while one was open for 4% of the time, Pallas kernels for 11%

profile of v4, /device:TPU:0, one launch (start us, length us, event | category | flops | bytes accessed | tf_op | source)
XLA Modules:
  0.0 42.1 jit_solution(3847958183657800954)
XLA Ops:
  0.0 3.0 %collective-permute-start = (bf16[6,2560]{1,0:T(8,128)(2,1)}, bf16[6,2560]{1,0:T(8,128)(2,1)S(1)}, u32[]{:S(2)}, u32[]{:S(2)}) collective-permute-start(bf16[6,2560]{1,0:T(8,128)(2,1)} %param.7), channel_id=1, source_target_pairs={{0,16},{1,18},{2,20},{3,22},{4,17},{5,19},{6,21},{7,23},{8,24},{9,... | collective-permute-start | bytes 92168 | tf_op jit(solution)/shard_map/ppermute | solution.py:395
  3.0 1.5 %collective-permute-start.1 = (bf16[6,2560]{1,0:T(8,128)(2,1)}, bf16[6,2560]{1,0:T(8,128)(2,1)S(1)}, u32[]{:S(2)}, u32[]{:S(2)}) collective-permute-start(bf16[6,2560]{1,0:T(8,128)(2,1)} %param.7), channel_id=1, source_target_pairs={{0,8},{1,10},{2,12},{3,14},{4,9},{5,11},{6,13},{7,15},{8,16},{9,18... | collective-permute-start | bytes 92168 | tf_op jit(solution)/shard_map/ppermute | solution.py:395
  4.5 1.4 %collective-permute-start.2 = (bf16[6,2560]{1,0:T(8,128)(2,1)}, bf16[6,2560]{1,0:T(8,128)(2,1)S(1)}, u32[]{:S(2)}, u32[]{:S(2)}) collective-permute-start(bf16[6,2560]{1,0:T(8,128)(2,1)} %param.7), channel_id=1, source_target_pairs={{0,0},{1,2},{2,4},{3,6},{4,1},{5,3},{6,5},{7,7},{8,8},{9,10},{10,1... | collective-permute-start | bytes 92168 | tf_op jit(solution)/shard_map/ppermute | solution.py:395
  5.9 0.0 collective-permute-done
  5.9 2.2 %collective-permute-done.1 = bf16[6,2560]{1,0:T(8,128)(2,1)S(1)} collective-permute-done((bf16[6,2560]{1,0:T(8,128)(2,1)}, bf16[6,2560]{1,0:T(8,128)(2,1)S(1)}, u32[]{:S(2)}, u32[]{:S(2)}) %collective-permute-start.1) | collective-permute-done | bytes 30752 | tf_op jit(solution)/shard_map/ppermute | solution.py:395
  8.1 0.0 collective-permute-done.2
  8.1 5.0 %collective-permute-start.3 = (bf16[3,6,2560]{2,1,0:T(8,128)(2,1)S(1)}, bf16[3,6,2560]{2,1,0:T(8,128)(2,1)S(1)}, u32[]{:S(2)}, u32[]{:S(2)}) collective-permute-start(bf16[3,6,2560]{2,1,0:T(8,128)(2,1)S(1)} %get-tuple-element.18.own_ref), channel_id=1, source_target_pairs={{0,1},{1,0},{2,3},{3,2},{4,5},{5,4},{6,7},{7,6},{8,9},{9,8},{10,11... | collective-permute-start | bytes 276488 | tf_op jit(solution)/shard_map/ppermute | solution.py:397
  13.1 1.0 %collective-permute-done.3.other_ref = bf16[3,6,2560]{2,1,0:T(8,128)(2,1)S(1)} collective-permute-done((bf16[3,6,2560]{2,1,0:T(8,128)(2,1)S(1)}, bf16[3,6,2560]{2,1,0:T(8,128)(2,1)S(1)}, u32[]{:S(2)}, u32[]{:S(2)}) %collective-permute-start.3) | collective-permute-done | bytes 92192 | tf_op jit(solution)/shard_map/ppermute | solution.py:397
  14.1 0.1 fusion
  14.2 0.0 collective-permute-start.4
  14.2 1.1 %band.1 = (bf16[640,768]{1,0:T(8,128)(2,1)S(1)}, f32[4,384]{1,0:T(4,128)S(1)}) custom-call(bf16[432,384]{1,0:T(8,128)(2,1)} %w_ref.1, f32[384]{0:T(512)} %refs_0_.1, f32[384]{0:T(512)} %refs_1_.1, f32[384]{0:T(512)} %refs_2_.1, f32[384]{0:T(512)} %refs_3_.1), custom_call_target="tpu_custom_call" | custom-call | tf_op jit(solution)/shard_map/band/pallas_call | solution.py:378
  15.4 0.7 %collective-permute-done.4.halo_ref = bf16[2,3,2,2560]{3,2,1,0:T(2,128)(2,1)S(1)} collective-permute-done((bf16[2,3,2,2560]{3,2,1,0:T(2,128)(2,1)S(1)}, bf16[2,3,2,2560]{3,2,1,0:T(2,128)(2,1)S(1)}, u32[]{:S(2)}, u32[]{:S(2)}) %collective-permute-start.4) | collective-permute-done | bytes 61472 | tf_op jit(solution)/shard_map/ppermute | solution.py:401
  16.1 2.1 %stats.1 = f32[32,1,128]{2,1,0:T(1,128)} custom-call(bf16[3,6,2560]{2,1,0:T(8,128)(2,1)S(1)} %get-tuple-element.18.own_ref, bf16[3,6,2560]{2,1,0:T(8,128)(2,1)S(1)} %collective-permute-done.3.other_ref, bf16[2,3,2,2560]{3,2,1,0:T(2,128)(2,1)S(1)} %collective-permute-done.4.halo_ref, bf16[640,768]{1,0:T(8,128)(2,1)S(1)} %get-tuple-element.11.band_ref, ...), custom_call_target="tpu_custom_call" | custom-call | tf_op jit(solution)/shard_map/stats/pallas_call | solution.py:415
  18.2 4.9 %all-to-all-start = ((f32[32,1,128]{2,1,0:T(1,128)}), f32[32,1,128]{2,1,0:T(1,128)S(1)}, u32[]{:S(2)}, u32[]{:S(2)}) async-start(f32[32,1,128]{2,1,0:T(1,128)} %stats.1), calls=%async_computation | async-start | bytes 32768 | tf_op jit(solution)/shard_map/all_to_all | solution.py:424
  23.1 3.6 %opened.1 = (f32[5,10,16,384]{3,2,1,0:T(8,128)S(1)}, f32[3,5,10,16,384]{4,3,2,1,0:T(8,128)}) custom-call(bf16[3,6,2560]{2,1,0:T(8,128)(2,1)S(1)} %get-tuple-element.18.own_ref, bf16[3,6,2560]{2,1,0:T(8,128)(2,1)S(1)} %collective-permute-done.3.other_ref, bf16[2,3,2,2560]{3,2,1,0:T(2,128)(2,1)S(1)} %collective-permute-done.4.halo_ref, ...), custom_call_target="tpu_custom_call" | custom-call | flops 1572864000 | bytes 4915200 | tf_op jit(solution)/shard_map/opened/pallas_call | solution.py:427
  26.7 1.7 %slice.3.head_ref = bf16[2304,384]{1,0:T(8,128)(2,1)S(1)} slice(bf16[10368,384]{1,0:T(8,128)(2,1)} %w_hbm.1), slice={[0:2304], [0:384]} | slice | bytes 3538944 | tf_op jit(solution)/shard_map/slice | solution.py:440
  28.4 1.8 %all-to-all-done.sum_ref = f32[32,1,128]{2,1,0:T(1,128)S(1)} async-done(((f32[32,1,128]{2,1,0:T(1,128)}), f32[32,1,128]{2,1,0:T(1,128)S(1)}, u32[]{:S(2)}, u32[]{:S(2)}) %all-to-all-start) | async-done | bytes 16416 | tf_op jit(solution)/shard_map/all_to_all | solution.py:424
  30.2 11.9 %second.1 = bf16[2,3,160,384]{3,2,1,0:T(8,128)(2,1)} custom-call(f32[32,1,128]{2,1,0:T(1,128)S(1)} %all-to-all-done.sum_ref, f32[5,10,16,384]{3,2,1,0:T(8,128)S(1)} %get-tuple-element.14.first_ref, f32[3,5,10,16,384]{4,3,2,1,0:T(8,128)} %get-tuple-element.15.o_hbm, bf16[2304,384]{1,0:T(8,128)(2,1)S(1)} %slice.3.head_ref, bf16[10368,384]{1,0:T(8,128)(2,1)} %w_hbm.1, ...), custom_call_target="tpu_custom_call" | custom-call | tf_op jit(solution)/shard_map/second/pallas_call | solution.py:351
  (1 shorter events, 0.0 us)
Async XLA Ops:
  0.0 5.9 %collective-permute-start = (bf16[6,2560]{1,0:T(8,128)(2,1)}, bf16[6,2560]{1,0:T(8,128)(2,1)S(1)}, u32[]{:S(2)}, u32[]{:S(2)}) collective-permute-start(bf16[6,2560]{1,0:T(8,128)(2,1)} %param.7), channel_id=1, source_target_pairs={{0,16},{1,18},{2,20},{3,22},{4,17},{5,19},{6,21},{7,23},{8,24},{9,... | collective-permute-start | bytes 92168 | tf_op jit(solution)/shard_map/ppermute | solution.py:395
  3.0 5.1 %collective-permute-start.1 = (bf16[6,2560]{1,0:T(8,128)(2,1)}, bf16[6,2560]{1,0:T(8,128)(2,1)S(1)}, u32[]{:S(2)}, u32[]{:S(2)}) collective-permute-start(bf16[6,2560]{1,0:T(8,128)(2,1)} %param.7), channel_id=1, source_target_pairs={{0,8},{1,10},{2,12},{3,14},{4,9},{5,11},{6,13},{7,15},{8,16},{9,18... | collective-permute-start | bytes 92168 | tf_op jit(solution)/shard_map/ppermute | solution.py:395
  4.5 3.6 %collective-permute-start.2 = (bf16[6,2560]{1,0:T(8,128)(2,1)}, bf16[6,2560]{1,0:T(8,128)(2,1)S(1)}, u32[]{:S(2)}, u32[]{:S(2)}) collective-permute-start(bf16[6,2560]{1,0:T(8,128)(2,1)} %param.7), channel_id=1, source_target_pairs={{0,0},{1,2},{2,4},{3,6},{4,1},{5,3},{6,5},{7,7},{8,8},{9,10},{10,1... | collective-permute-start | bytes 92168 | tf_op jit(solution)/shard_map/ppermute | solution.py:395
  8.1 6.0 %collective-permute-start.3 = (bf16[3,6,2560]{2,1,0:T(8,128)(2,1)S(1)}, bf16[3,6,2560]{2,1,0:T(8,128)(2,1)S(1)}, u32[]{:S(2)}, u32[]{:S(2)}) collective-permute-start(bf16[3,6,2560]{2,1,0:T(8,128)(2,1)S(1)} %get-tuple-element.18.own_ref), channel_id=1, source_target_pairs={{0,1},{1,0},{2,3},{3,2},{4,5},{5,4},{6,7},{7,6},{8,9},{9,8},{10,11... | collective-permute-start | bytes 276488 | tf_op jit(solution)/shard_map/ppermute | solution.py:397
  14.2 1.9 %collective-permute-start.4 = (bf16[2,3,2,2560]{3,2,1,0:T(2,128)(2,1)S(1)}, bf16[2,3,2,2560]{3,2,1,0:T(2,128)(2,1)S(1)}, u32[]{:S(2)}, u32[]{:S(2)}) collective-permute-start(bf16[2,3,2,2560]{3,2,1,0:T(2,128)(2,1)S(1)} %fusion), channel_id=1, source_target_pairs={{0,2},{2,4},{4,6},{6,7},{3,1},{5,3},{7,5},{1,0},{8,10},{10,12},{12... | collective-permute-start | bytes 184328 | tf_op jit(solution)/shard_map/ppermute | solution.py:401
  18.2 12.0 %all-to-all-start = ((f32[32,1,128]{2,1,0:T(1,128)}), f32[32,1,128]{2,1,0:T(1,128)S(1)}, u32[]{:S(2)}, u32[]{:S(2)}) async-start(f32[32,1,128]{2,1,0:T(1,128)} %stats.1), calls=%async_computation | async-start | bytes 32768 | tf_op jit(solution)/shard_map/all_to_all | solution.py:424

commit v5 on v4

--- a/solution.py
+++ b/solution.py
@@ -330,12 +330,13 @@
     rows1, rows2, rows3 = (act_rows(t) for t in (1, 2, 3))
     act(0)
     wait1 = functools.partial(need, weights[0], loads[0])
-    wait2 = functools.partial(need, *weights[1:4], loads[1])
+    wait2 = functools.partial(need, *weights[1:4])
+    arrived = functools.partial(need, loads[1])
     wait3 = functools.partial(need, *weights[4:], loads[2])
     wait3a = functools.partial(need, *weights[4:])
     wait3b = functools.partial(need, loads[2])
     edge(0, 0, [((0, 1), steps([], [], [wait1])), ((2,), steps(rows1, [wait2]))])
-    shared(1, steps(rows2, [wait3]))
+    shared(1, steps([], [arrived, wait3], rows2))
     shared(2, steps(rows3))
     first = finish(0)
     edge(1, 2, [((0, 1, 2), [])])

time: 42.3 us -> 42.2 us (level)
  no operation moved by 1% of the time
where the time goes in v5:
time: 42.2 us; the launch traced here: 42 us
  Pallas kernels  18.6 us (44%)
  starting transfers between devices  15.8 us (37%)
  waiting for transfers between devices  5.7 us (14%)
  local copies, waits for them, and re-layouts  1.66 us (4%)
    pallas_call x1, Pallas kernels, second_part(): pl.pallas_call(functools.partial(second_kernel, rows, entries), out_shape...  11.8 us
    ppermute x3, starting transfers between devices, shards(): received.append(lax.ppermute(latent, ('tm', 'height'), route))  5.91 us
    ppermute x1, starting transfers between devices, shards(): other = lax.ppermute(own, 'height', [(i, i ^ 1) for i in range(height)])  5 us
    all_to_all x1, starting transfers between devices, shards(): sums = lax.all_to_all(sums, ('tm', 'height'), 0, 0, tiled=True)  4.88 us
    pallas_call x1, Pallas kernels, shards(): pl.pallas_call(functools.partial(opened_kernel, rows), out_shape=(pltpu.V...  3.63 us
    ppermute x3, waiting for transfers between devices, shards(): received.append(lax.ppermute(latent, ('tm', 'height'), route))  2.2 us
    pallas_call x1, Pallas kernels, shards(): pl.pallas_call(functools.partial(stats_kernel, rows), out_shape=jax.Shape...  2.09 us
    all_to_all x1, waiting for transfers between devices, shards(): sums = lax.all_to_all(sums, ('tm', 'height'), 0, 0, tiled=True)  1.8 us
  transfers between devices with their start and end apart: 6, of which 4 were waited for; matrix products, arithmetic and copies ran while one was open for 4% of the time, Pallas kernels for 11%

profile of v5, /device:TPU:0, one launch (start us, length us, event | category | flops | bytes accessed | tf_op | source)
XLA Modules:
  0.0 42.0 jit_solution(9319383930907670182)
XLA Ops:
  0.0 3.0 %collective-permute-start = (bf16[6,2560]{1,0:T(8,128)(2,1)}, bf16[6,2560]{1,0:T(8,128)(2,1)S(1)}, u32[]{:S(2)}, u32[]{:S(2)}) collective-permute-start(bf16[6,2560]{1,0:T(8,128)(2,1)} %param.7), channel_id=1, source_target_pairs={{0,16},{1,18},{2,20},{3,22},{4,17},{5,19},{6,21},{7,23},{8,24},{9,... | collective-permute-start | bytes 92168 | tf_op jit(solution)/shard_map/ppermute | solution.py:396
  3.0 1.5 %collective-permute-start.1 = (bf16[6,2560]{1,0:T(8,128)(2,1)}, bf16[6,2560]{1,0:T(8,128)(2,1)S(1)}, u32[]{:S(2)}, u32[]{:S(2)}) collective-permute-start(bf16[6,2560]{1,0:T(8,128)(2,1)} %param.7), channel_id=1, source_target_pairs={{0,8},{1,10},{2,12},{3,14},{4,9},{5,11},{6,13},{7,15},{8,16},{9,18... | collective-permute-start | bytes 92168 | tf_op jit(solution)/shard_map/ppermute | solution.py:396
  4.5 1.4 %collective-permute-start.2 = (bf16[6,2560]{1,0:T(8,128)(2,1)}, bf16[6,2560]{1,0:T(8,128)(2,1)S(1)}, u32[]{:S(2)}, u32[]{:S(2)}) collective-permute-start(bf16[6,2560]{1,0:T(8,128)(2,1)} %param.7), channel_id=1, source_target_pairs={{0,0},{1,2},{2,4},{3,6},{4,1},{5,3},{6,5},{7,7},{8,8},{9,10},{10,1... | collective-permute-start | bytes 92168 | tf_op jit(solution)/shard_map/ppermute | solution.py:396
  5.9 0.0 collective-permute-done
  5.9 2.2 %collective-permute-done.1 = bf16[6,2560]{1,0:T(8,128)(2,1)S(1)} collective-permute-done((bf16[6,2560]{1,0:T(8,128)(2,1)}, bf16[6,2560]{1,0:T(8,128)(2,1)S(1)}, u32[]{:S(2)}, u32[]{:S(2)}) %collective-permute-start.1) | collective-permute-done | bytes 30752 | tf_op jit(solution)/shard_map/ppermute | solution.py:396
  8.1 0.0 collective-permute-done.2
  8.1 5.0 %collective-permute-start.3 = (bf16[3,6,2560]{2,1,0:T(8,128)(2,1)S(1)}, bf16[3,6,2560]{2,1,0:T(8,128)(2,1)S(1)}, u32[]{:S(2)}, u32[]{:S(2)}) collective-permute-start(bf16[3,6,2560]{2,1,0:T(8,128)(2,1)S(1)} %get-tuple-element.18.own_ref), channel_id=1, source_target_pairs={{0,1},{1,0},{2,3},{3,2},{4,5},{5,4},{6,7},{7,6},{8,9},{9,8},{10,11... | collective-permute-start | bytes 276488 | tf_op jit(solution)/shard_map/ppermute | solution.py:398
  13.1 1.0 %collective-permute-done.3.other_ref = bf16[3,6,2560]{2,1,0:T(8,128)(2,1)S(1)} collective-permute-done((bf16[3,6,2560]{2,1,0:T(8,128)(2,1)S(1)}, bf16[3,6,2560]{2,1,0:T(8,128)(2,1)S(1)}, u32[]{:S(2)}, u32[]{:S(2)}) %collective-permute-start.3) | collective-permute-done | bytes 92192 | tf_op jit(solution)/shard_map/ppermute | solution.py:398
  14.1 0.1 fusion
  14.2 0.0 collective-permute-start.4
  14.2 1.1 %band.1 = (bf16[640,768]{1,0:T(8,128)(2,1)S(1)}, f32[4,384]{1,0:T(4,128)S(1)}) custom-call(bf16[432,384]{1,0:T(8,128)(2,1)} %w_ref.1, f32[384]{0:T(512)} %refs_0_.1, f32[384]{0:T(512)} %refs_1_.1, f32[384]{0:T(512)} %refs_2_.1, f32[384]{0:T(512)} %refs_3_.1), custom_call_target="tpu_custom_call" | custom-call | tf_op jit(solution)/shard_map/band/pallas_call | solution.py:379
  15.4 0.7 %collective-permute-done.4.halo_ref = bf16[2,3,2,2560]{3,2,1,0:T(2,128)(2,1)S(1)} collective-permute-done((bf16[2,3,2,2560]{3,2,1,0:T(2,128)(2,1)S(1)}, bf16[2,3,2,2560]{3,2,1,0:T(2,128)(2,1)S(1)}, u32[]{:S(2)}, u32[]{:S(2)}) %collective-permute-start.4) | collective-permute-done | bytes 61472 | tf_op jit(solution)/shard_map/ppermute | solution.py:402
  16.1 2.1 %stats.1 = f32[32,1,128]{2,1,0:T(1,128)} custom-call(bf16[3,6,2560]{2,1,0:T(8,128)(2,1)S(1)} %get-tuple-element.18.own_ref, bf16[3,6,2560]{2,1,0:T(8,128)(2,1)S(1)} %collective-permute-done.3.other_ref, bf16[2,3,2,2560]{3,2,1,0:T(2,128)(2,1)S(1)} %collective-permute-done.4.halo_ref, bf16[640,768]{1,0:T(8,128)(2,1)S(1)} %get-tuple-element.11.band_ref, ...), custom_call_target="tpu_custom_call" | custom-call | tf_op jit(solution)/shard_map/stats/pallas_call | solution.py:416
  18.2 4.9 %all-to-all-start = ((f32[32,1,128]{2,1,0:T(1,128)}), f32[32,1,128]{2,1,0:T(1,128)S(1)}, u32[]{:S(2)}, u32[]{:S(2)}) async-start(f32[32,1,128]{2,1,0:T(1,128)} %stats.1), calls=%async_computation | async-start | bytes 32768 | tf_op jit(solution)/shard_map/all_to_all | solution.py:425
  23.1 3.6 %opened.1 = (f32[5,10,16,384]{3,2,1,0:T(8,128)S(1)}, f32[3,5,10,16,384]{4,3,2,1,0:T(8,128)}) custom-call(bf16[3,6,2560]{2,1,0:T(8,128)(2,1)S(1)} %get-tuple-element.18.own_ref, bf16[3,6,2560]{2,1,0:T(8,128)(2,1)S(1)} %collective-permute-done.3.other_ref, bf16[2,3,2,2560]{3,2,1,0:T(2,128)(2,1)S(1)} %collective-permute-done.4.halo_ref, ...), custom_call_target="tpu_custom_call" | custom-call | flops 1572864000 | bytes 4915200 | tf_op jit(solution)/shard_map/opened/pallas_call | solution.py:428
  26.7 1.7 %slice.3.head_ref = bf16[2304,384]{1,0:T(8,128)(2,1)S(1)} slice(bf16[10368,384]{1,0:T(8,128)(2,1)} %w_hbm.1), slice={[0:2304], [0:384]} | slice | bytes 3538944 | tf_op jit(solution)/shard_map/slice | solution.py:441
  28.4 1.8 %all-to-all-done.sum_ref = f32[32,1,128]{2,1,0:T(1,128)S(1)} async-done(((f32[32,1,128]{2,1,0:T(1,128)}), f32[32,1,128]{2,1,0:T(1,128)S(1)}, u32[]{:S(2)}, u32[]{:S(2)}) %all-to-all-start) | async-done | bytes 16416 | tf_op jit(solution)/shard_map/all_to_all | solution.py:425
  30.2 11.8 %second.1 = bf16[2,3,160,384]{3,2,1,0:T(8,128)(2,1)} custom-call(f32[32,1,128]{2,1,0:T(1,128)S(1)} %all-to-all-done.sum_ref, f32[5,10,16,384]{3,2,1,0:T(8,128)S(1)} %get-tuple-element.14.first_ref, f32[3,5,10,16,384]{4,3,2,1,0:T(8,128)} %get-tuple-element.15.o_hbm, bf16[2304,384]{1,0:T(8,128)(2,1)S(1)} %slice.3.head_ref, bf16[10368,384]{1,0:T(8,128)(2,1)} %w_hbm.1, ...), custom_call_target="tpu_custom_call" | custom-call | tf_op jit(solution)/shard_map/second/pallas_call | solution.py:352
  (1 shorter events, 0.0 us)
Async XLA Ops:
  0.0 5.9 %collective-permute-start = (bf16[6,2560]{1,0:T(8,128)(2,1)}, bf16[6,2560]{1,0:T(8,128)(2,1)S(1)}, u32[]{:S(2)}, u32[]{:S(2)}) collective-permute-start(bf16[6,2560]{1,0:T(8,128)(2,1)} %param.7), channel_id=1, source_target_pairs={{0,16},{1,18},{2,20},{3,22},{4,17},{5,19},{6,21},{7,23},{8,24},{9,... | collective-permute-start | bytes 92168 | tf_op jit(solution)/shard_map/ppermute | solution.py:396
  3.0 5.1 %collective-permute-start.1 = (bf16[6,2560]{1,0:T(8,128)(2,1)}, bf16[6,2560]{1,0:T(8,128)(2,1)S(1)}, u32[]{:S(2)}, u32[]{:S(2)}) collective-permute-start(bf16[6,2560]{1,0:T(8,128)(2,1)} %param.7), channel_id=1, source_target_pairs={{0,8},{1,10},{2,12},{3,14},{4,9},{5,11},{6,13},{7,15},{8,16},{9,18... | collective-permute-start | bytes 92168 | tf_op jit(solution)/shard_map/ppermute | solution.py:396
  4.5 3.6 %collective-permute-start.2 = (bf16[6,2560]{1,0:T(8,128)(2,1)}, bf16[6,2560]{1,0:T(8,128)(2,1)S(1)}, u32[]{:S(2)}, u32[]{:S(2)}) collective-permute-start(bf16[6,2560]{1,0:T(8,128)(2,1)} %param.7), channel_id=1, source_target_pairs={{0,0},{1,2},{2,4},{3,6},{4,1},{5,3},{6,5},{7,7},{8,8},{9,10},{10,1... | collective-permute-start | bytes 92168 | tf_op jit(solution)/shard_map/ppermute | solution.py:396
  8.1 6.0 %collective-permute-start.3 = (bf16[3,6,2560]{2,1,0:T(8,128)(2,1)S(1)}, bf16[3,6,2560]{2,1,0:T(8,128)(2,1)S(1)}, u32[]{:S(2)}, u32[]{:S(2)}) collective-permute-start(bf16[3,6,2560]{2,1,0:T(8,128)(2,1)S(1)} %get-tuple-element.18.own_ref), channel_id=1, source_target_pairs={{0,1},{1,0},{2,3},{3,2},{4,5},{5,4},{6,7},{7,6},{8,9},{9,8},{10,11... | collective-permute-start | bytes 276488 | tf_op jit(solution)/shard_map/ppermute | solution.py:398
  14.2 1.9 %collective-permute-start.4 = (bf16[2,3,2,2560]{3,2,1,0:T(2,128)(2,1)S(1)}, bf16[2,3,2,2560]{3,2,1,0:T(2,128)(2,1)S(1)}, u32[]{:S(2)}, u32[]{:S(2)}) collective-permute-start(bf16[2,3,2,2560]{3,2,1,0:T(2,128)(2,1)S(1)} %fusion), channel_id=1, source_target_pairs={{0,2},{2,4},{4,6},{6,7},{3,1},{5,3},{7,5},{1,0},{8,10},{10,12},{12... | collective-permute-start | bytes 184328 | tf_op jit(solution)/shard_map/ppermute | solution.py:402
  18.2 12.0 %all-to-all-start = ((f32[32,1,128]{2,1,0:T(1,128)}), f32[32,1,128]{2,1,0:T(1,128)S(1)}, u32[]{:S(2)}, u32[]{:S(2)}) async-start(f32[32,1,128]{2,1,0:T(1,128)} %stats.1), calls=%async_computation | async-start | bytes 32768 | tf_op jit(solution)/shard_map/all_to_all | solution.py:425

commit v6 on v4

--- a/solution.py
+++ b/solution.py
@@ -62,10 +62,8 @@
             for half in range(2):
                 z_ref[half, row : row + SEG, :] = jnp.zeros((SEG, LANES), F32)
 
-    def spread(piece, frame, slot):
-        base = pl.multiple_of((frame * slots + slot) * SEG, SEG)
-        count = piece.shape[0]
-        edge = jnp.zeros((count, LANES), F32)
+    def spread(piece, frame, *places):
+        edge = jnp.zeros((piece.shape[0], LANES), F32)
         wide = jnp.concatenate([edge, piece, edge, edge], axis=1)
         for s in range(SEG):
             for half in range(2):
@@ -74,7 +72,11 @@
                 window = wide[:, lo : lo + 2 * LANES]
                 if start > lo:
                     window = pltpu.roll(window, 2 * LANES - (start - lo), 1)
-                z_ref[half, pl.ds(base + s, count, stride=SEG), :] = window[:, :LANES]
+                done = 0
+                for count, slot in places:
+                    base = pl.multiple_of((frame * slots + slot) * SEG, SEG)
+                    z_ref[half, pl.ds(base + s, count, stride=SEG), :] = window[done : done + count, :LANES]
+                    done += count
 
     main = jnp.where(core == 0, rows, 0)
     edge_slot = jnp.where(core == 0, rows - 2, 2 * rows)
@@ -86,10 +88,10 @@
         def piece(ref, keep, *index):
             return jnp.where(keep, ref[(*index, d)].astype(F32), 0.0)
 
-        spread(piece(own_ref, real), 2 * d + core, main)
-        spread(piece(other_ref, real), 2 * d + 1 - core, main)
-        spread(piece(halo_ref, real & beside, 0), 2 * d + core, edge_slot)
-        spread(piece(halo_ref, real & beside, 1), 2 * d + 1 - core, edge_slot)
+        places = ((2 * rows, main), (2, edge_slot))
+        for ref, side, frame in ((own_ref, 0, 2 * d + core), (other_ref, 1, 2 * d + 1 - core)):
+            both = jnp.concatenate([piece(ref, real), piece(halo_ref, real & beside, side)], axis=0)
+            spread(both, frame, *places)
 
     first = rows - 2
     span = rows + 4

time: 42.3 us -> 42.2 us (level)
  no operation moved by 1% of the time
where the time goes in v6:
time: 42.2 us; the launch traced here: 41.9 us
  Pallas kernels  18.5 us (44%)
  starting transfers between devices  15.8 us (37%)
  waiting for transfers between devices  5.8 us (14%)
  local copies, waits for them, and re-layouts  1.66 us (4%)
    pallas_call x1, Pallas kernels, second_part(): pl.pallas_call(functools.partial(second_kernel, rows, entries), out_shape...  11.9 us
    ppermute x3, starting transfers between devices, shards(): received.append(lax.ppermute(latent, ('tm', 'height'), route))  5.91 us
    ppermute x1, starting transfers between devices, shards(): other = lax.ppermute(own, 'height', [(i, i ^ 1) for i in range(height)])  5 us
    all_to_all x1, starting transfers between devices, shards(): sums = lax.all_to_all(sums, ('tm', 'height'), 0, 0, tiled=True)  4.88 us
    pallas_call x1, Pallas kernels, shards(): pl.pallas_call(functools.partial(opened_kernel, rows), out_shape=(pltpu.V...  3.53 us
    ppermute x3, waiting for transfers between devices, shards(): received.append(lax.ppermute(latent, ('tm', 'height'), route))  2.2 us
    pallas_call x1, Pallas kernels, shards(): pl.pallas_call(functools.partial(stats_kernel, rows), out_shape=jax.Shape...  1.95 us
    all_to_all x1, waiting for transfers between devices, shards(): sums = lax.all_to_all(sums, ('tm', 'height'), 0, 0, tiled=True)  1.9 us
  transfers between devices with their start and end apart: 6, of which 4 were waited for; matrix products, arithmetic and copies ran while one was open for 4% of the time, Pallas kernels for 11%

profile of v6, /device:TPU:0, one launch (start us, length us, event | category | flops | bytes accessed | tf_op | source)
XLA Modules:
  0.0 41.9 jit_solution(6818498077964298324)
XLA Ops:
  0.0 3.0 %collective-permute-start = (bf16[6,2560]{1,0:T(8,128)(2,1)}, bf16[6,2560]{1,0:T(8,128)(2,1)S(1)}, u32[]{:S(2)}, u32[]{:S(2)}) collective-permute-start(bf16[6,2560]{1,0:T(8,128)(2,1)} %param.7), channel_id=1, source_target_pairs={{0,16},{1,18},{2,20},{3,22},{4,17},{5,19},{6,21},{7,23},{8,24},{9,... | collective-permute-start | bytes 92168 | tf_op jit(solution)/shard_map/ppermute | solution.py:397
  3.0 1.5 %collective-permute-start.1 = (bf16[6,2560]{1,0:T(8,128)(2,1)}, bf16[6,2560]{1,0:T(8,128)(2,1)S(1)}, u32[]{:S(2)}, u32[]{:S(2)}) collective-permute-start(bf16[6,2560]{1,0:T(8,128)(2,1)} %param.7), channel_id=1, source_target_pairs={{0,8},{1,10},{2,12},{3,14},{4,9},{5,11},{6,13},{7,15},{8,16},{9,18... | collective-permute-start | bytes 92168 | tf_op jit(solution)/shard_map/ppermute | solution.py:397
  4.5 1.4 %collective-permute-start.2 = (bf16[6,2560]{1,0:T(8,128)(2,1)}, bf16[6,2560]{1,0:T(8,128)(2,1)S(1)}, u32[]{:S(2)}, u32[]{:S(2)}) collective-permute-start(bf16[6,2560]{1,0:T(8,128)(2,1)} %param.7), channel_id=1, source_target_pairs={{0,0},{1,2},{2,4},{3,6},{4,1},{5,3},{6,5},{7,7},{8,8},{9,10},{10,1... | collective-permute-start | bytes 92168 | tf_op jit(solution)/shard_map/ppermute | solution.py:397
  5.9 0.0 collective-permute-done
  5.9 2.2 %collective-permute-done.1 = bf16[6,2560]{1,0:T(8,128)(2,1)S(1)} collective-permute-done((bf16[6,2560]{1,0:T(8,128)(2,1)}, bf16[6,2560]{1,0:T(8,128)(2,1)S(1)}, u32[]{:S(2)}, u32[]{:S(2)}) %collective-permute-start.1) | collective-permute-done | bytes 30752 | tf_op jit(solution)/shard_map/ppermute | solution.py:397
  8.1 0.0 collective-permute-done.2
  8.1 5.0 %collective-permute-start.3 = (bf16[3,6,2560]{2,1,0:T(8,128)(2,1)S(1)}, bf16[3,6,2560]{2,1,0:T(8,128)(2,1)S(1)}, u32[]{:S(2)}, u32[]{:S(2)}) collective-permute-start(bf16[3,6,2560]{2,1,0:T(8,128)(2,1)S(1)} %get-tuple-element.18.own_ref), channel_id=1, source_target_pairs={{0,1},{1,0},{2,3},{3,2},{4,5},{5,4},{6,7},{7,6},{8,9},{9,8},{10,11... | collective-permute-start | bytes 276488 | tf_op jit(solution)/shard_map/ppermute | solution.py:399
  13.1 1.0 %collective-permute-done.3.other_ref = bf16[3,6,2560]{2,1,0:T(8,128)(2,1)S(1)} collective-permute-done((bf16[3,6,2560]{2,1,0:T(8,128)(2,1)S(1)}, bf16[3,6,2560]{2,1,0:T(8,128)(2,1)S(1)}, u32[]{:S(2)}, u32[]{:S(2)}) %collective-permute-start.3) | collective-permute-done | bytes 92192 | tf_op jit(solution)/shard_map/ppermute | solution.py:399
  14.1 0.1 fusion
  14.2 0.0 collective-permute-start.4
  14.2 1.1 %band.1 = (bf16[640,768]{1,0:T(8,128)(2,1)S(1)}, f32[4,384]{1,0:T(4,128)S(1)}) custom-call(bf16[432,384]{1,0:T(8,128)(2,1)} %w_ref.1, f32[384]{0:T(512)} %refs_0_.1, f32[384]{0:T(512)} %refs_1_.1, f32[384]{0:T(512)} %refs_2_.1, f32[384]{0:T(512)} %refs_3_.1), custom_call_target="tpu_custom_call" | custom-call | tf_op jit(solution)/shard_map/band/pallas_call | solution.py:380
  15.4 0.7 %collective-permute-done.4.halo_ref = bf16[2,3,2,2560]{3,2,1,0:T(2,128)(2,1)S(1)} collective-permute-done((bf16[2,3,2,2560]{3,2,1,0:T(2,128)(2,1)S(1)}, bf16[2,3,2,2560]{3,2,1,0:T(2,128)(2,1)S(1)}, u32[]{:S(2)}, u32[]{:S(2)}) %collective-permute-start.4) | collective-permute-done | bytes 61472 | tf_op jit(solution)/shard_map/ppermute | solution.py:403
  16.1 1.9 %stats.1 = f32[32,1,128]{2,1,0:T(1,128)} custom-call(bf16[3,6,2560]{2,1,0:T(8,128)(2,1)S(1)} %get-tuple-element.18.own_ref, bf16[3,6,2560]{2,1,0:T(8,128)(2,1)S(1)} %collective-permute-done.3.other_ref, bf16[2,3,2,2560]{3,2,1,0:T(2,128)(2,1)S(1)} %collective-permute-done.4.halo_ref, bf16[640,768]{1,0:T(8,128)(2,1)S(1)} %get-tuple-element.11.band_ref, ...), custom_call_target="tpu_custom_call" | custom-call | tf_op jit(solution)/shard_map/stats/pallas_call | solution.py:417
  18.0 4.9 %all-to-all-start = ((f32[32,1,128]{2,1,0:T(1,128)}), f32[32,1,128]{2,1,0:T(1,128)S(1)}, u32[]{:S(2)}, u32[]{:S(2)}) async-start(f32[32,1,128]{2,1,0:T(1,128)} %stats.1), calls=%async_computation | async-start | bytes 32768 | tf_op jit(solution)/shard_map/all_to_all | solution.py:426
  22.9 3.5 %opened.1 = (f32[5,10,16,384]{3,2,1,0:T(8,128)S(1)}, f32[3,5,10,16,384]{4,3,2,1,0:T(8,128)}) custom-call(bf16[3,6,2560]{2,1,0:T(8,128)(2,1)S(1)} %get-tuple-element.18.own_ref, bf16[3,6,2560]{2,1,0:T(8,128)(2,1)S(1)} %collective-permute-done.3.other_ref, bf16[2,3,2,2560]{3,2,1,0:T(2,128)(2,1)S(1)} %collective-permute-done.4.halo_ref, ...), custom_call_target="tpu_custom_call" | custom-call | flops 1572864000 | bytes 4915200 | tf_op jit(solution)/shard_map/opened/pallas_call | solution.py:429
  26.5 1.7 %slice.3.head_ref = bf16[2304,384]{1,0:T(8,128)(2,1)S(1)} slice(bf16[10368,384]{1,0:T(8,128)(2,1)} %w_hbm.1), slice={[0:2304], [0:384]} | slice | bytes 3538944 | tf_op jit(solution)/shard_map/slice | solution.py:442
  28.1 1.9 %all-to-all-done.sum_ref = f32[32,1,128]{2,1,0:T(1,128)S(1)} async-done(((f32[32,1,128]{2,1,0:T(1,128)}), f32[32,1,128]{2,1,0:T(1,128)S(1)}, u32[]{:S(2)}, u32[]{:S(2)}) %all-to-all-start) | async-done | bytes 16416 | tf_op jit(solution)/shard_map/all_to_all | solution.py:426
  30.0 11.9 %second.1 = bf16[2,3,160,384]{3,2,1,0:T(8,128)(2,1)} custom-call(f32[32,1,128]{2,1,0:T(1,128)S(1)} %all-to-all-done.sum_ref, f32[5,10,16,384]{3,2,1,0:T(8,128)S(1)} %get-tuple-element.14.first_ref, f32[3,5,10,16,384]{4,3,2,1,0:T(8,128)} %get-tuple-element.15.o_hbm, bf16[2304,384]{1,0:T(8,128)(2,1)S(1)} %slice.3.head_ref, bf16[10368,384]{1,0:T(8,128)(2,1)} %w_hbm.1, ...), custom_call_target="tpu_custom_call" | custom-call | tf_op jit(solution)/shard_map/second/pallas_call | solution.py:353
  (1 shorter events, 0.0 us)
Async XLA Ops:
  0.0 5.9 %collective-permute-start = (bf16[6,2560]{1,0:T(8,128)(2,1)}, bf16[6,2560]{1,0:T(8,128)(2,1)S(1)}, u32[]{:S(2)}, u32[]{:S(2)}) collective-permute-start(bf16[6,2560]{1,0:T(8,128)(2,1)} %param.7), channel_id=1, source_target_pairs={{0,16},{1,18},{2,20},{3,22},{4,17},{5,19},{6,21},{7,23},{8,24},{9,... | collective-permute-start | bytes 92168 | tf_op jit(solution)/shard_map/ppermute | solution.py:397
  3.0 5.1 %collective-permute-start.1 = (bf16[6,2560]{1,0:T(8,128)(2,1)}, bf16[6,2560]{1,0:T(8,128)(2,1)S(1)}, u32[]{:S(2)}, u32[]{:S(2)}) collective-permute-start(bf16[6,2560]{1,0:T(8,128)(2,1)} %param.7), channel_id=1, source_target_pairs={{0,8},{1,10},{2,12},{3,14},{4,9},{5,11},{6,13},{7,15},{8,16},{9,18... | collective-permute-start | bytes 92168 | tf_op jit(solution)/shard_map/ppermute | solution.py:397
  4.5 3.6 %collective-permute-start.2 = (bf16[6,2560]{1,0:T(8,128)(2,1)}, bf16[6,2560]{1,0:T(8,128)(2,1)S(1)}, u32[]{:S(2)}, u32[]{:S(2)}) collective-permute-start(bf16[6,2560]{1,0:T(8,128)(2,1)} %param.7), channel_id=1, source_target_pairs={{0,0},{1,2},{2,4},{3,6},{4,1},{5,3},{6,5},{7,7},{8,8},{9,10},{10,1... | collective-permute-start | bytes 92168 | tf_op jit(solution)/shard_map/ppermute | solution.py:397
  8.1 6.0 %collective-permute-start.3 = (bf16[3,6,2560]{2,1,0:T(8,128)(2,1)S(1)}, bf16[3,6,2560]{2,1,0:T(8,128)(2,1)S(1)}, u32[]{:S(2)}, u32[]{:S(2)}) collective-permute-start(bf16[3,6,2560]{2,1,0:T(8,128)(2,1)S(1)} %get-tuple-element.18.own_ref), channel_id=1, source_target_pairs={{0,1},{1,0},{2,3},{3,2},{4,5},{5,4},{6,7},{7,6},{8,9},{9,8},{10,11... | collective-permute-start | bytes 276488 | tf_op jit(solution)/shard_map/ppermute | solution.py:399
  14.2 1.9 %collective-permute-start.4 = (bf16[2,3,2,2560]{3,2,1,0:T(2,128)(2,1)S(1)}, bf16[2,3,2,2560]{3,2,1,0:T(2,128)(2,1)S(1)}, u32[]{:S(2)}, u32[]{:S(2)}) collective-permute-start(bf16[2,3,2,2560]{3,2,1,0:T(2,128)(2,1)S(1)} %fusion), channel_id=1, source_target_pairs={{0,2},{2,4},{4,6},{6,7},{3,1},{5,3},{7,5},{1,0},{8,10},{10,12},{12... | collective-permute-start | bytes 184328 | tf_op jit(solution)/shard_map/ppermute | solution.py:403
  18.0 12.0 %all-to-all-start = ((f32[32,1,128]{2,1,0:T(1,128)}), f32[32,1,128]{2,1,0:T(1,128)S(1)}, u32[]{:S(2)}, u32[]{:S(2)}) async-start(f32[32,1,128]{2,1,0:T(1,128)} %stats.1), calls=%async_computation | async-start | bytes 32768 | tf_op jit(solution)/shard_map/all_to_all | solution.py:426
